TPU v7x, 256 devices: a whole 4x4x8 slice. The times are simulated.
256 devices in a mesh: exp: 32 (over x, z), dat: 8 (over y, core).
Axes of the slice: x: 4, y: 4, z: 8, core: 2. Of those that a mesh axis runs over, the one named last changes fastest.
Arguments:
- tokens: bfloat16 [32768, 1024], P(('exp', 'dat')), may hold values from -6 to 6
- norm_gain: float32 [1024], replicated, may hold values from 0.25 to 1.75
- router_weight: bfloat16 [1024, 128], P(None, 'exp'), may hold values from -0.1875 to 0.1875
- inner_weight: bfloat16 [128, 1024, 4096], P('exp', None, 'dat'), may hold values from -0.1875 to 0.1875
- outer_weight: bfloat16 [128, 4096, 1024], P('exp', 'dat'), may hold values from -0.09375 to 0.09375
- slot_tokens: int32 [128, 512], P('exp', 'dat'), may hold values from 0 to 32767, as said below
- slot_ids: int32 [32768, 2], P(('exp', 'dat')), may hold values from 0 to 65535, as said below
Outputs:
- mixed: bfloat16 [32768, 1024], P(('exp', 'dat'))
Inputs may be any that keep to these rules, and one draw needn't show every extreme that they name: `slot_tokens`: column c of an expert names only tokens of the devices whose dat index is c // 64; one expert names no token twice. The 256 slots of the experts of one exp index in one dat group name tokens of any one device at most 24 times, exactly 24 times for some devices, and no times for some. Every token is named by exactly 2 slots. slot_ids[t] holds the two slots e * 512 + c with slot_tokens[e, c] = t, the smaller first.
All inputs are finite; a program needn't handle non-finite values.
Results may differ from a plain program's by a relative error of at most 0.0085.
Values may be sent and summed in bfloat16 or wider, within the bound.
A program may use at most 64 MiB of HBM per device.

v0:
```python
import jax
import jax.numpy as jnp
from jax import lax
from jax.sharding import PartitionSpec as P

EPSILON = 1e-06


def normalize(tokens, norm_gain):
    values = tokens.astype(jnp.float32)
    scale = lax.rsqrt(jnp.mean(values * values, axis=-1, keepdims=True) + EPSILON)
    return (values * scale * norm_gain).astype(jnp.bfloat16)


def owner_places(slot_ids, experts_dev, capacity, bucket):
    flat_ids = slot_ids.reshape(-1)
    source = flat_ids // capacity // experts_dev
    before = (source[:, None] == source[None, :]) & (flat_ids[None, :] < flat_ids[:, None])
    ranks_in = jnp.sum(before.astype(jnp.int32), axis=1)
    return (source * bucket + ranks_in).reshape(slot_ids.shape)


def expert_places(token_ids, slot_keys, tok_rows, dat_count, bucket):
    owner_of = token_ids // (tok_rows * dat_count)
    before = (owner_of[:, None] == owner_of[None, :]) & (slot_keys[None, :] < slot_keys[:, None])
    ranks_in = jnp.sum(before.astype(jnp.int32), axis=1)
    return owner_of * bucket + ranks_in


def body(tokens, norm_gain, router_weight, inner_weight, outer_weight, slot_tokens, slot_ids):
    exp_count = lax.axis_size("exp")
    dat_count = lax.axis_size("dat")
    tok_rows, width = tokens.shape
    experts_dev, cap_dev = slot_tokens.shape
    bucket = 6 * tok_rows // exp_count
    normed = normalize(tokens, norm_gain)
    picked = slot_tokens.T.reshape(-1)
    expert_iota = lax.broadcasted_iota(jnp.int32, (cap_dev, experts_dev), 1)
    column_iota = lax.broadcasted_iota(jnp.int32, (cap_dev, experts_dev), 0)
    slot_keys = (expert_iota * cap_dev + column_iota).reshape(-1)
    senders = expert_places(picked, slot_keys, tok_rows, dat_count, bucket)
    receivers = owner_places(slot_ids, experts_dev, cap_dev * dat_count, bucket)
    lookup = jnp.any(
        lax.broadcasted_iota(jnp.int32, (exp_count * bucket, 1, 1), 0) == receivers[None], axis=2
    )
    outgoing = jnp.dot(lookup.astype(jnp.bfloat16), normed, preferred_element_type=jnp.float32)
    outgoing = outgoing.astype(jnp.bfloat16).reshape(exp_count, bucket, width)
    arrived = lax.all_to_all(outgoing, "exp", split_axis=0, concat_axis=0, tiled=True).reshape(
        exp_count * bucket, width
    )
    gathered_rows = jnp.take(arrived, senders, axis=0)
    gathered_rows = gathered_rows.reshape(cap_dev, experts_dev, width)
    gate_score = jax.nn.sigmoid(
        jnp.einsum("ced,de->ce", gathered_rows, router_weight, preferred_element_type=jnp.float32)
    )
    inner = jnp.einsum(
        "ced,edf->cef",
        lax.all_gather(gathered_rows, "dat", axis=0, tiled=True),
        inner_weight,
        preferred_element_type=jnp.float32,
    )
    hidden = jax.nn.relu(inner).astype(jnp.bfloat16)
    expert_out = lax.psum_scatter(
        jnp.einsum("cef,efd->ced", hidden, outer_weight, preferred_element_type=jnp.float32).astype(
            jnp.bfloat16
        ),
        "dat",
        scatter_dimension=0,
        tiled=True,
    ).astype(jnp.float32)
    weighted = (gate_score[:, :, None] * expert_out).astype(jnp.bfloat16).reshape(-1, width)
    placing = lax.broadcasted_iota(jnp.int32, (exp_count * bucket, 1), 0) == senders[None, :]
    returning = jnp.dot(placing.astype(jnp.bfloat16), weighted, preferred_element_type=jnp.float32)
    returning = returning.astype(jnp.bfloat16).reshape(exp_count, bucket, width)
    came_back = lax.all_to_all(returning, "exp", split_axis=0, concat_axis=0, tiled=True).reshape(
        exp_count * bucket, width
    )
    combine_table = jnp.sum(
        (
            lax.broadcasted_iota(jnp.int32, (1, 1, exp_count * bucket), 2) == receivers[:, :, None]
        ).astype(jnp.float32),
        axis=1,
    )
    combined = jnp.dot(
        combine_table.astype(jnp.bfloat16), came_back, preferred_element_type=jnp.float32
    )
    return (tokens.astype(jnp.float32) + combined).astype(jnp.bfloat16)


def solution(mesh):
    in_specs = (
        P(("exp", "dat"), None),
        P(),
        P(None, "exp"),
        P("exp", None, "dat"),
        P("exp", "dat", None),
        P("exp", "dat"),
        P(("exp", "dat"), None),
    )
    out_specs = P(("exp", "dat"), None)
    return jax.shard_map(body, mesh=mesh, in_specs=in_specs, out_specs=out_specs, check_vma=False)
```

profile of v0, /device:TPU:8, one launch (start us, length us, event | category | flops | bytes accessed | tf_op | source)
XLA Modules:
  0.0 207.2 jit_solution(4173374861839967735)
XLA Ops:
  6.5 0.0 copy-start
  6.5 0.0 copy-start.3
  6.5 0.8 copy.45
  7.4 0.1 reshape.373
  7.5 0.2 convert_reduce_fusion.2
  7.7 0.1 reduce_sum.43
  7.9 0.1 copy.46
  7.9 0.7 multiply_add_fusion.1
  8.7 0.1 fusion.10
  8.8 1.1 fusion.11
  9.8 2.8 %convolution_convert_fusion = bf16[768,1024]{1,0:T(8,128)(2,1)} fusion(pred[768,128]{1,0:T(8,128)(4,1)S(1)} %fusion.10, bf16[128,1024]{1,0:T(8,128)(2,1)} %param.7, f32[1024]{0:T(1024)} %param.8, f32[128]{0:T(128)S(1)} %add_rsqrt_fusion), kind=kOutput, calls=%fused_computation.6 | convolution fusion | flops 202637312 | bytes 1937920 | tf_op jit(solution)/shard_map/dot_general | solution.py:46
  12.6 11.3 %all-to-all-start = ((bf16[32,24,1024]{2,1,0:T(8,128)(2,1)}), bf16[32,24,1024]{2,1,0:T(8,128)(2,1)S(1)}, u32[]{:S(2)}, u32[]{:S(2)}) async-start(bf16[32,24,1024]{2,1,0:T(8,128)(2,1)} %bitcast.1), calls=%async_computation | async-start | bytes 3145728 | tf_op jit(solution)/shard_map/all_to_all | solution.py:48
  23.9 0.0 all-gather.2.cloned.1.call-start
  24.0 0.0 copy-done.3
  24.0 0.1 copy.47
  24.1 0.1 reshape.374
  24.2 0.1 reshape.377
  24.3 0.1 add.133
  24.4 0.2 convert_reduce_fusion.1
  24.7 0.1 reduce_sum.46
  24.8 0.1 copy.48
  24.9 0.1 copy.49
  25.0 38.2 %all-to-all-done = bf16[32,24,1024]{2,1,0:T(8,128)(2,1)S(1)} async-done(((bf16[32,24,1024]{2,1,0:T(8,128)(2,1)}), bf16[32,24,1024]{2,1,0:T(8,128)(2,1)S(1)}, u32[]{:S(2)}, u32[]{:S(2)}) %all-to-all-start) | async-done | bytes 1572896 | tf_op jit(solution)/shard_map/all_to_all | solution.py:48
  63.3 1.2 gather_fusion
  64.4 0.2 gather.7
  64.6 1.2 broadcast_select_fusion
  65.8 0.0 all-gather.2.cloned.1.call-update
  65.8 0.0 reduce-scatter.2.cloned.1.call-start
  65.9 30.9 %all-gather.2.cloned.1.call-done = bf16[512,4,1024]{2,1,0:T(4,128)(2,1)} async-done(((bf16[64,4,1024]{2,1,0:T(4,128)(2,1)}), bf16[512,4,1024]{2,1,0:T(4,128)(2,1)}) %all-gather.2.cloned.1.call-update) | async-done | bytes 4194320 | tf_op jit(solution)/shard_map/all_gather | solution.py:58
  96.7 11.5 %convert_bitcast_fusion = bf16[512,4,1024]{2,0,1:T(8,128)(2,1)} fusion(bf16[4,512,1024]{2,1,0:T(8,128)(2,1)} %param.11, bf16[4,1024,512]{2,1,0:T(8,128)(2,1)} %param.10, bf16[512,4,1024]{2,1,0:T(4,128)(2,1)} %all-gather.2.cloned.1.call-done), kind=kOutput, calls=%fused_computation.3 | convolution fusion | flops 4299161600 | bytes 16777216 | tf_op jit(solution)/shard_map/cef,efd->ced/dot_general | solution.py:64
  108.3 0.0 copy-start.2
  108.3 0.0 reduce-scatter.2.cloned.1.call-update
  108.3 0.0 copy-done
  108.3 1.0 copy-done.2
  109.3 0.3 fusion.14
  109.6 0.0 copy-start.1
  109.6 36.9 %reduce-scatter.2.cloned.1.call-done = bf16[64,4,1024]{2,0,1:T(8,128)(2,1)} async-done(((bf16[512,4,1024]{2,0,1:T(8,128)(2,1)}), bf16[64,4,1024]{2,0,1:T(8,128)(2,1)}) %reduce-scatter.2.cloned.1.call-update) | async-done | bytes 524304 | tf_op jit(solution)/shard_map/reduce_scatter | solution.py:63
  146.5 1.2 multiply_convert_fusion
  147.6 0.4 copy.52
  148.1 0.1 reshape.378
  148.2 1.7 convolution_convert_fusion.1
  149.9 9.9 %all-to-all-start.1 = ((bf16[32,24,1024]{2,1,0:T(8,128)(2,1)}), bf16[32,24,1024]{2,1,0:T(8,128)(2,1)S(1)}, u32[]{:S(2)}, u32[]{:S(2)}) async-start(bf16[32,24,1024]{2,1,0:T(8,128)(2,1)} %bitcast.11), calls=%async_computation.2 | async-start | bytes 3145728 | tf_op jit(solution)/shard_map/all_to_all | solution.py:75
  159.8 0.1 convert_reduce_fusion
  159.9 39.4 %all-to-all-done.1 = bf16[32,24,1024]{2,1,0:T(8,128)(2,1)S(1)} async-done(((bf16[32,24,1024]{2,1,0:T(8,128)(2,1)}), bf16[32,24,1024]{2,1,0:T(8,128)(2,1)S(1)}, u32[]{:S(2)}, u32[]{:S(2)}) %all-to-all-start.1) | async-done | bytes 1572896 | tf_op jit(solution)/shard_map/all_to_all | solution.py:75
  199.3 0.0 copy-done.1
  199.3 1.1 fusion.5
  (10 shorter events, 0.1 us)
Async XLA Ops:
  6.5 101.8 %copy-start = (bf16[1024,4]{0,1:T(4,128)(2,1)S(1)}, bf16[1024,4]{0,1:T(4,128)(2,1)}, u32[]{:S(2)}) copy-start(bf16[1024,4]{0,1:T(4,128)(2,1)} %param.9) | copy-start | bytes 24580
  6.5 17.4 %copy-start.3 = (s32[4,64]{1,0:T(4,128)S(1)}, s32[4,64]{1,0:T(4,128)}, u32[]{:S(2)}) copy-start(s32[4,64]{1,0:T(4,128)} %param.12) | copy-start | bytes 3076
  12.6 50.7 %all-to-all-start = ((bf16[32,24,1024]{2,1,0:T(8,128)(2,1)}), bf16[32,24,1024]{2,1,0:T(8,128)(2,1)S(1)}, u32[]{:S(2)}, u32[]{:S(2)}) async-start(bf16[32,24,1024]{2,1,0:T(8,128)(2,1)} %bitcast.1), calls=%async_computation | async-start | bytes 3145728 | tf_op jit(solution)/shard_map/all_to_all | solution.py:48
  23.9 72.8 %all-gather.2.cloned.1.call-start = ((), (), s32[]{:S(2)}) async-start(), calls=%async_computation.3 | async-start | bytes 4718592 | tf_op jit(solution)/shard_map/all_gather | solution.py:58
  65.8 80.6 %reduce-scatter.2.cloned.1.call-start = ((), (), s32[]{:S(2)}) async-start(), calls=%async_computation.4 | async-start | bytes 4718592 | tf_op jit(solution)/shard_map/reduce_scatter | solution.py:63
  108.3 1.0 copy-start.2
  109.6 89.7 %copy-start.1 = (bf16[128,1024]{1,0:T(8,128)(2,1)S(1)}, bf16[128,1024]{1,0:T(8,128)(2,1)}, u32[]{:S(2)}) copy-start(bf16[128,1024]{1,0:T(8,128)(2,1)} %param.7) | copy-start | bytes 786436
  149.9 49.4 %all-to-all-start.1 = ((bf16[32,24,1024]{2,1,0:T(8,128)(2,1)}), bf16[32,24,1024]{2,1,0:T(8,128)(2,1)S(1)}, u32[]{:S(2)}, u32[]{:S(2)}) async-start(bf16[32,24,1024]{2,1,0:T(8,128)(2,1)} %bitcast.11), calls=%async_computation.2 | async-start | bytes 3145728 | tf_op jit(solution)/shard_map/all_to_all | solution.py:75
Sparse Core Ops, SparseCore 0:
  66.0 30.7 all-gather.1
  108.4 37.9 reduce-scatter.1
where the time goes:
time: 208 us; the launch traced here: 207 us
  waiting for transfers between devices  145 us (70%)
  starting transfers between devices  21.2 us (10%)
  matrix products  17.3 us (8%)
  between operations  13.6 us (7%)
  other arithmetic  4.93 us (2%)
  local copies, waits for them, and re-layouts  4.75 us (2%)
    all_to_all x1, waiting for transfers between devices, body(): lax.all_to_all(returning, 'exp', split_axis=0, concat_axis=0, tiled=True)  39.4 us
    all_to_all x1, waiting for transfers between devices, body(): lax.all_to_all(outgoing, 'exp', split_axis=0, concat_axis=0, tiled=True)  38.2 us
    reduce_scatter x1, waiting for transfers between devices, body(): lax.psum_scatter(jnp.einsum('cef,efd->ced', hidden, outer_weight, preferr...  36.9 us
    all_gather x1, waiting for transfers between devices, body(): lax.all_gather(gathered_rows, 'dat', axis=0, tiled=True)  30.9 us
    dot_general x1, matrix products, body(): jnp.einsum('cef,efd->ced', hidden, outer_weight, preferred_element_type=j...  11.5 us
    all_to_all x1, starting transfers between devices, body(): lax.all_to_all(outgoing, 'exp', split_axis=0, concat_axis=0, tiled=True)  11.3 us
    all_to_all x1, starting transfers between devices, body(): lax.all_to_all(returning, 'exp', split_axis=0, concat_axis=0, tiled=True)  9.85 us
  transfers between devices with their start and end apart: 4, of which 4 were waited for; matrix products, arithmetic and copies ran while one was open for 1% of the time, Pallas kernels for 0%

commit v1 on v0

v1 whole, which is shorter than its diff:
```python
import functools

import jax
import jax.numpy as jnp
from jax import lax
from jax.experimental import pallas as pl
from jax.experimental.pallas import tpu as pltpu
from jax.sharding import PartitionSpec as P

EPSILON = 1e-06
MESH = pl.DeviceIdType.MESH
BF16 = jnp.bfloat16
F32 = jnp.float32


def normalize(tokens, norm_gain):
    values = tokens.astype(jnp.float32)
    scale = lax.rsqrt(jnp.mean(values * values, axis=-1, keepdims=True) + EPSILON)
    return (values * scale * norm_gain).astype(jnp.bfloat16)


def owner_places(slot_ids, experts_dev, capacity, bucket):
    flat_ids = slot_ids.reshape(-1)
    source = flat_ids // capacity // experts_dev
    before = (source[:, None] == source[None, :]) & (flat_ids[None, :] < flat_ids[:, None])
    ranks_in = jnp.sum(before.astype(jnp.int32), axis=1)
    return (source * bucket + ranks_in).reshape(slot_ids.shape)


def expert_places(token_ids, slot_keys, tok_rows, dat_count, bucket):
    owner_of = token_ids // (tok_rows * dat_count)
    before = (owner_of[:, None] == owner_of[None, :]) & (slot_keys[None, :] < slot_keys[:, None])
    ranks_in = jnp.sum(before.astype(jnp.int32), axis=1)
    return owner_of * bucket + ranks_in


def ffn_kernel(
    rows, router, w1_hbm, w2_hbm, out,
    X, W1, W2, PS, R, S, T, F,
    w_sem, sendP, recvP, sendI, recvI, rsend, rrecv, fsend, frecv, tsend, trecv,
):
    experts, C, width = rows.shape
    dat = lax.axis_index("dat")
    c, y = dat % 2, dat // 2
    partner = y * 2 + (1 - c)
    plus = ((y + 1) % 4) * 2 + c
    minus = ((y + 3) % 4) * 2 + c
    half = experts // 2

    weights = []
    for e in range(experts):
        weights.append(pltpu.make_async_copy(w1_hbm.at[e], W1.at[e], w_sem.at[0, e]))
        weights.append(pltpu.make_async_copy(w2_hbm.at[e], W2.at[e], w_sem.at[1, e]))
    for copy in weights:
        copy.start()

    barrier = pltpu.get_barrier_semaphore()
    for other in (partner, plus, minus):
        pl.semaphore_signal(barrier, inc=1, device_id={"dat": other}, device_id_type=MESH)
    pl.semaphore_wait(barrier, 3)

    def remote(src, dst, send, recv, where):
        return pltpu.make_async_remote_copy(
            src_ref=src, dst_ref=dst, send_sem=send, recv_sem=recv, device_id={"dat": where}, device_id_type=MESH
        )

    own = pl.ds(0, C)
    other_rows = pl.ds(C, C)

    def to_plus(e):
        return remote(rows.at[e], X.at[1, e, own], sendI.at[1, e], recvI.at[1, e], plus)

    def to_minus(e):
        return remote(rows.at[e], X.at[2, e, own], sendI.at[2, e], recvI.at[2, e], minus)

    def to_partner(s, e):
        src = rows.at[e] if s == 0 else X.at[s, e, own]
        return remote(src, X.at[s, e, other_rows], sendP.at[s, e], recvP.at[s, e], partner)

    def onward(e):
        if e < half:
            return remote(X.at[1, e, own], X.at[3, e, own], sendI.at[3, e], recvI.at[3, e], plus)
        return remote(X.at[2, e, own], X.at[3, e, own], sendI.at[3, e], recvI.at[3, e], minus)

    def part_to_partner(s, e):
        return remote(PS.at[s, e, other_rows], R.at[s, e], rsend.at[s, e], rrecv.at[s, e], partner)

    def final_plus(e):
        return remote(S.at[2, e], F.at[0, e], fsend.at[0, e], frecv.at[0, e], plus)

    def final_minus(e):
        return remote(S.at[1, e], F.at[1, e], fsend.at[1, e], frecv.at[1, e], minus)

    def transit(e):
        where = plus if e < half else minus
        return remote(S.at[3, e], T.at[e], tsend.at[e], trecv.at[e], where)

    def ffn(s, e):
        inner = jnp.dot(X[s, e], W1[e], preferred_element_type=F32)
        hidden = jnp.maximum(inner, 0.0).astype(BF16)
        PS[s, e] = jnp.dot(hidden, W2[e], preferred_element_type=F32).astype(BF16)

    def chip_sum(s, e):
        part_to_partner(s, e).wait_recv()
        return PS[s, e, :C].astype(F32) + R[s, e].astype(F32)

    for k in range(experts):
        to_plus(k).start()
        to_minus((k + half) % experts).start()
    for k in range(experts):
        to_partner(0, k).start()
    for e in range(experts):
        X[0, e, :C] = rows[e]

    def first(e, carry):
        remote(rows.at[e], X.at[0, e, other_rows], sendP.at[0, e], recvP.at[0, e], partner).wait_recv()
        pltpu.make_async_copy(w1_hbm.at[e], W1.at[e], w_sem.at[0, e]).wait()
        pltpu.make_async_copy(w2_hbm.at[e], W2.at[e], w_sem.at[1, e]).wait()
        ffn(0, e)
        part_to_partner(0, e).start()
        return carry

    lax.fori_loop(0, experts, first, 0)

    def arrivals(k):
        if k < experts:
            return [(1, k), (2, (k + half) % experts)]
        if k < experts + half:
            return [(3, k - experts), (3, k - experts + half)]
        return []

    def receive(s, e):
        src = rows.at[e] if s < 3 else X.at[1, e, own]
        remote(src, X.at[s, e, own], sendI.at[s, e], recvI.at[s, e], partner).wait_recv()
        to_partner(s, e).start()
        if (s == 1 and e < half) or (s == 2 and e >= half):
            onward(e).start()

    def compute(pairs):
        for s, e in pairs:
            to_partner(s, e).wait_recv()
        (s0, e0), (s1, e1) = pairs

        def one(i, carry):
            ffn(s0 + (s1 - s0) * i, e0 + (e1 - e0) * i)
            return carry

        lax.fori_loop(0, 2, one, 0)
        for s, e in pairs:
            part_to_partner(s, e).start()

    def settle(pairs):
        for s, e in pairs:
            S[s, e] = chip_sum(s, e).astype(BF16)
            if s == 3:
                transit(e).start()
            elif s == 1 and e < half:
                final_minus(e).start()
            elif s == 2 and e >= half:
                final_plus(e).start()

    for k in range(experts + half + 2):
        for s, e in arrivals(k):
            receive(s, e)
        if k >= 1 and arrivals(k - 1):
            compute(arrivals(k - 1))
        if k >= 2 and arrivals(k - 2):
            settle(arrivals(k - 2))

    for k in range(half):
        a, b = k, k + half
        transit(a).wait_recv()
        S[2, a] = (S[2, a].astype(F32) + T[a].astype(F32)).astype(BF16)
        final_plus(a).start()
        transit(b).wait_recv()
        S[1, b] = (S[1, b].astype(F32) + T[b].astype(F32)).astype(BF16)
        final_minus(b).start()

    for e in list(range(half, experts)) + list(range(half)):
        logits = jnp.sum(rows[e].astype(F32) * router[e : e + 1].astype(F32), axis=1, keepdims=True)
        gate = jax.nn.sigmoid(logits)
        total = chip_sum(0, e)
        final_plus(e).wait_recv()
        final_minus(e).wait_recv()
        total = total + F[0, e].astype(F32) + F[1, e].astype(F32)
        out[e] = (gate * total).astype(BF16)

    for e in range(experts):
        to_plus(e).wait_send()
        to_minus(e).wait_send()
        onward(e).wait_send()
        final_plus(e).wait_send()
        final_minus(e).wait_send()
        transit(e).wait_send()
        for s in range(4):
            to_partner(s, e).wait_send()
            part_to_partner(s, e).wait_send()


def expert_layer(rows, router, inner_weight, outer_weight):
    experts, C, width = rows.shape
    hidden = inner_weight.shape[2]
    dma = pltpu.SemaphoreType.DMA
    vmem = pl.BlockSpec(memory_space=pltpu.VMEM)
    hbm = pl.BlockSpec(memory_space=pl.ANY)
    return pl.pallas_call(
        ffn_kernel,
        name="expert_layer",
        out_shape=jax.ShapeDtypeStruct((experts, C, width), BF16),
        in_specs=[vmem, vmem, hbm, hbm],
        out_specs=vmem,
        scratch_shapes=[
            pltpu.VMEM((4, experts, 2 * C, width), BF16),
            pltpu.VMEM((experts, width, hidden), BF16),
            pltpu.VMEM((experts, hidden, width), BF16),
            pltpu.VMEM((4, experts, 2 * C, width), BF16),
            pltpu.VMEM((4, experts, C, width), BF16),
            pltpu.VMEM((4, experts, C, width), BF16),
            pltpu.VMEM((experts, C, width), BF16),
            pltpu.VMEM((2, experts, C, width), BF16),
            dma((2, experts)),
            dma((4, experts)),
            dma((4, experts)),
            dma((4, experts)),
            dma((4, experts)),
            dma((4, experts)),
            dma((4, experts)),
            dma((2, experts)),
            dma((2, experts)),
            dma((experts,)),
            dma((experts,)),
        ],
        compiler_params=pltpu.CompilerParams(
            collective_id=0, has_side_effects=True, vmem_limit_bytes=60 * 1024 * 1024
        ),
    )(rows, router, inner_weight, outer_weight)


def body(tokens, norm_gain, router_weight, inner_weight, outer_weight, slot_tokens, slot_ids):
    exp_count = lax.axis_size("exp")
    dat_count = lax.axis_size("dat")
    tok_rows, width = tokens.shape
    experts_dev, cap_dev = slot_tokens.shape
    bucket = 6 * tok_rows // exp_count
    normed = normalize(tokens, norm_gain)
    picked = slot_tokens.reshape(-1)
    slot_keys = lax.iota(jnp.int32, experts_dev * cap_dev)
    senders = expert_places(picked, slot_keys, tok_rows, dat_count, bucket)
    receivers = owner_places(slot_ids, experts_dev, cap_dev * dat_count, bucket)
    lookup = jnp.any(
        lax.broadcasted_iota(jnp.int32, (exp_count * bucket, 1, 1), 0) == receivers[None], axis=2
    )
    outgoing = jnp.dot(lookup.astype(BF16), normed, preferred_element_type=F32)
    outgoing = outgoing.astype(BF16).reshape(exp_count, bucket, width)
    arrived = lax.all_to_all(outgoing, "exp", split_axis=0, concat_axis=0, tiled=True).reshape(
        exp_count * bucket, width
    )
    placing = lax.broadcasted_iota(jnp.int32, (exp_count * bucket, 1), 0) == senders[None, :]
    placing = placing.astype(BF16)
    gathered_rows = lax.dot_general(
        placing, arrived, (((0,), (0,)), ((), ())), preferred_element_type=F32
    ).astype(BF16)
    gathered_rows = gathered_rows.reshape(experts_dev, cap_dev, width)
    weighted = expert_layer(gathered_rows, router_weight.T, inner_weight, outer_weight)
    weighted = weighted.reshape(-1, width)
    returning = jnp.dot(placing, weighted, preferred_element_type=F32)
    returning = returning.astype(BF16).reshape(exp_count, bucket, width)
    came_back = lax.all_to_all(returning, "exp", split_axis=0, concat_axis=0, tiled=True).reshape(
        exp_count * bucket, width
    )
    combine_table = jnp.sum(
        (lax.broadcasted_iota(jnp.int32, (1, 1, exp_count * bucket), 2) == receivers[:, :, None]).astype(F32),
        axis=1,
    )
    combined = jnp.dot(combine_table.astype(BF16), came_back, preferred_element_type=F32)
    return (tokens.astype(F32) + combined).astype(BF16)


def solution(mesh):
    in_specs = (
        P(("exp", "dat"), None),
        P(),
        P(None, "exp"),
        P("exp", None, "dat"),
        P("exp", "dat", None),
        P("exp", "dat"),
        P(("exp", "dat"), None),
    )
    out_specs = P(("exp", "dat"), None)
    return jax.shard_map(body, mesh=mesh, in_specs=in_specs, out_specs=out_specs, check_vma=False)
```

time: 208 us -> 150 us (0.72); the launches traced: 207 us -> 147 us
  waiting for transfers between devices: 145 us -> 77.3 us
  Pallas kernels: 0 us -> 40.5 us
  between operations: 13.6 us -> 0.08 us
  matrix products: 17.3 us -> 8.03 us
  starting transfers between devices: 21.2 us -> 17.4 us
  local copies, waits for them, and re-layouts: 4.75 us -> 1.21 us
  other arithmetic: 4.93 us -> 2.47 us
    pallas_call x0 -> x1, Pallas kernels: none -> 40.5 us  [expert_layer(): pl.pallas_call(ffn_kernel, name='expert_layer', out_shape=jax.ShapeDtypeS...]
    reduce_scatter x1 -> x0, waiting for transfers between devices: 36.9 us -> none  [body(): lax.psum_scatter(jnp.einsum('cef,efd->ced', hidden, outer_weight, preferr...]
    all_gather x1 -> x0, waiting for transfers between devices: 30.9 us -> none  [body(): lax.all_gather(gathered_rows, 'dat', axis=0, tiled=True)]
    dot_general x5 -> x4, matrix products: 17.3 us -> 8.03 us  [the longest x1 2.78 us: body(): returning = jnp.dot(placing, weighted, preferred_element_type=F32)]
    all_to_all x1, starting transfers between devices: 9.85 us -> 5.93 us  [body(): lax.all_to_all(returning, 'exp', split_axis=0, concat_axis=0, tiled=True)]
  transfers between devices with their start and end apart: 4 -> 2, of which waited for: 4 -> 2; matrix products, arithmetic and copies ran while one was open for 1% -> 0% of each run, Pallas kernels for 0% -> 0%
where the time goes in v1:
time: 150 us; the launch traced here: 147 us
  waiting for transfers between devices  77.3 us (52%)
  Pallas kernels  40.5 us (27%)
  starting transfers between devices  17.4 us (12%)
  matrix products  8.03 us (5%)
  other arithmetic  2.47 us (2%)
    pallas_call x1, Pallas kernels, expert_layer(): pl.pallas_call(ffn_kernel, name='expert_layer', out_shape=jax.ShapeDtypeS...  40.5 us
    all_to_all x1, waiting for transfers between devices, body(): lax.all_to_all(outgoing, 'exp', split_axis=0, concat_axis=0, tiled=True)  39 us
    all_to_all x1, waiting for transfers between devices, body(): lax.all_to_all(returning, 'exp', split_axis=0, concat_axis=0, tiled=True)  38.2 us
    all_to_all x1, starting transfers between devices, body(): lax.all_to_all(outgoing, 'exp', split_axis=0, concat_axis=0, tiled=True)  11.4 us
    all_to_all x1, starting transfers between devices, body(): lax.all_to_all(returning, 'exp', split_axis=0, concat_axis=0, tiled=True)  5.93 us
  transfers between devices with their start and end apart: 2, of which 2 were waited for; matrix products, arithmetic and copies ran while one was open for 0% of the time, Pallas kernels for 0%

profile of v1, /device:TPU:8, one launch (start us, length us, event | category | flops | bytes accessed | tf_op | source)
XLA Modules:
  0.0 147.0 jit_solution(4678201458933240448)
XLA Ops:
  0.0 0.8 copy.28
  0.8 0.1 reshape.262
  0.9 0.2 convert_reduce_fusion.2
  1.2 0.1 reduce_sum.39
  1.3 0.1 copy.29
  1.4 0.7 multiply_add_fusion.1
  2.1 0.1 fusion.1
  2.2 1.1 fusion.2
  3.3 2.8 %convolution_convert_fusion = bf16[768,1024]{1,0:T(8,128)(2,1)} fusion(pred[768,128]{1,0:T(8,128)(4,1)S(1)} %fusion.1, bf16[128,1024]{1,0:T(8,128)(2,1)} %param.7, f32[1024]{0:T(1024)} %param.8, f32[128]{0:T(128)S(1)} %add_rsqrt_fusion), kind=kOutput, calls=%fused_computation | convolution fusion | flops 202637312 | bytes 1937920 | tf_op jit(solution)/shard_map/dot_general | solution.py:253
  6.0 0.0 copy-start.1
  6.0 11.4 %all-to-all-start = ((bf16[32,24,1024]{2,1,0:T(8,128)(2,1)}), bf16[32,24,1024]{2,1,0:T(8,128)(2,1)S(1)}, u32[]{:S(2)}, u32[]{:S(2)}) async-start(bf16[32,24,1024]{2,1,0:T(8,128)(2,1)} %bitcast), calls=%async_computation | async-start | bytes 3145728 | tf_op jit(solution)/shard_map/all_to_all | solution.py:255
  17.5 0.0 copy-done.1
  17.5 0.1 reshape.263
  17.6 0.2 convert_reduce_fusion.1
  17.8 39.0 %all-to-all-done = bf16[32,24,1024]{2,1,0:T(8,128)(2,1)S(1)} async-done(((bf16[32,24,1024]{2,1,0:T(8,128)(2,1)}), bf16[32,24,1024]{2,1,0:T(8,128)(2,1)S(1)}, u32[]{:S(2)}, u32[]{:S(2)}) %all-to-all-start) | async-done | bytes 1572896 | tf_op jit(solution)/shard_map/all_to_all | solution.py:255
  56.8 1.4 convolution_convert_fusion.2
  58.2 40.5 %expert_layer.1 = bf16[4,64,1024]{2,1,0:T(8,128)(2,1)} custom-call(bf16[4,64,1024]{2,1,0:T(8,128)(2,1)} %bitcast.15, bf16[4,1024]{1,0:T(4,128)(2,1)} %bitcast.16, bf16[4,1024,512]{2,1,0:T(8,128)(2,1)} %w1_hbm.1, bf16[4,512,1024]{2,1,0:T(8,128)(2,1)} %w2_hbm.1), custom_call_target="tpu_custom_call" | custom-call | tf_op jit(solution)/shard_map/expert_layer/pallas_call | solution.py:206
  98.8 2.8 %convolution_convert_fusion.1 = bf16[768,1024]{1,0:T(8,128)(2,1)} fusion(bf16[256,1024]{1,0:T(8,128)(2,1)} %bitcast.13, s32[256]{0:T(256)S(1)} %multiply_add_fusion), kind=kOutput, calls=%fused_computation.1 | convolution fusion | flops 403636224 | bytes 2098176 | tf_op jit(solution)/shard_map/dot_general | solution.py:266
  101.6 0.0 copy-start
  101.6 5.9 %all-to-all-start.1 = ((bf16[32,24,1024]{2,1,0:T(8,128)(2,1)}), bf16[32,24,1024]{2,1,0:T(8,128)(2,1)S(1)}, u32[]{:S(2)}, u32[]{:S(2)}) async-start(bf16[32,24,1024]{2,1,0:T(8,128)(2,1)} %bitcast.5), calls=%async_computation.1 | async-start | bytes 3145728 | tf_op jit(solution)/shard_map/all_to_all | solution.py:268
  107.5 0.1 convert_reduce_fusion
  107.6 38.2 %all-to-all-done.1 = bf16[32,24,1024]{2,1,0:T(8,128)(2,1)S(1)} async-done(((bf16[32,24,1024]{2,1,0:T(8,128)(2,1)}), bf16[32,24,1024]{2,1,0:T(8,128)(2,1)S(1)}, u32[]{:S(2)}, u32[]{:S(2)}) %all-to-all-start.1) | async-done | bytes 1572896 | tf_op jit(solution)/shard_map/all_to_all | solution.py:268
  145.9 0.0 copy-done
  145.9 1.1 fusion
  (4 shorter events, 0.1 us)
Async XLA Ops:
  6.0 11.5 %copy-start.1 = (s32[4,64]{1,0:T(4,128)S(1)}, s32[4,64]{1,0:T(4,128)}, u32[]{:S(2)}) copy-start(s32[4,64]{1,0:T(4,128)} %param.12) | copy-start | bytes 3076
  6.0 50.8 %all-to-all-start = ((bf16[32,24,1024]{2,1,0:T(8,128)(2,1)}), bf16[32,24,1024]{2,1,0:T(8,128)(2,1)S(1)}, u32[]{:S(2)}, u32[]{:S(2)}) async-start(bf16[32,24,1024]{2,1,0:T(8,128)(2,1)} %bitcast), calls=%async_computation | async-start | bytes 3145728 | tf_op jit(solution)/shard_map/all_to_all | solution.py:255
  101.6 44.3 %copy-start = (bf16[128,1024]{1,0:T(8,128)(2,1)S(1)}, bf16[128,1024]{1,0:T(8,128)(2,1)}, u32[]{:S(2)}) copy-start(bf16[128,1024]{1,0:T(8,128)(2,1)} %param.7) | copy-start | bytes 786436
  101.6 44.3 %all-to-all-start.1 = ((bf16[32,24,1024]{2,1,0:T(8,128)(2,1)}), bf16[32,24,1024]{2,1,0:T(8,128)(2,1)S(1)}, u32[]{:S(2)}, u32[]{:S(2)}) async-start(bf16[32,24,1024]{2,1,0:T(8,128)(2,1)} %bitcast.5), calls=%async_computation.1 | async-start | bytes 3145728 | tf_op jit(solution)/shard_map/all_to_all | solution.py:268

commit v2 on v1

--- a/solution.py
+++ b/solution.py
@@ -13,29 +13,259 @@
 F32 = jnp.float32
 
 
-def normalize(tokens, norm_gain):
-    values = tokens.astype(jnp.float32)
-    scale = lax.rsqrt(jnp.mean(values * values, axis=-1, keepdims=True) + EPSILON)
-    return (values * scale * norm_gain).astype(jnp.bfloat16)
-
-
-def owner_places(slot_ids, experts_dev, capacity, bucket):
-    flat_ids = slot_ids.reshape(-1)
-    source = flat_ids // capacity // experts_dev
-    before = (source[:, None] == source[None, :]) & (flat_ids[None, :] < flat_ids[:, None])
-    ranks_in = jnp.sum(before.astype(jnp.int32), axis=1)
-    return (source * bucket + ranks_in).reshape(slot_ids.shape)
-
-
-def expert_places(token_ids, slot_keys, tok_rows, dat_count, bucket):
-    owner_of = token_ids // (tok_rows * dat_count)
-    before = (owner_of[:, None] == owner_of[None, :]) & (slot_keys[None, :] < slot_keys[:, None])
-    ranks_in = jnp.sum(before.astype(jnp.int32), axis=1)
-    return owner_of * bucket + ranks_in
-
-
-def ffn_kernel(
-    rows, router, w1_hbm, w2_hbm, out,
+NX, NZ = 4, 8
+BUCKET = 24
+
+
+def dot(a, b):
+    return jnp.dot(a, b, preferred_element_type=F32)
+
+
+def lane_rows(column_code, width):
+    return jnp.transpose(jnp.broadcast_to(column_code, (width, width)))
+
+
+class Exchange:
+    def __init__(self, refs, width):
+        self.__dict__.update(refs)
+        exp = lax.axis_index("exp")
+        self.x, self.z = exp // NZ, exp % NZ
+        self.half = width // 2
+
+    def at(self, dx, dz):
+        return ((self.x + dx) % NX) * NZ + (self.z + dz) % NZ
+
+    def peers(self):
+        return [self.at(0, dz) for dz in range(1, NZ)] + [self.at(1, 0), self.at(NX - 1, 0)]
+
+    def remote(self, src, dst, send, recv, where):
+        return pltpu.make_async_remote_copy(
+            src_ref=src, dst_ref=dst, send_sem=send, recv_sem=recv, device_id={"exp": where}, device_id_type=MESH
+        )
+
+    def cols(self, h):
+        return pl.ds(h * self.half, self.half)
+
+    def spread(self, j, h, up):
+        src = self.G.at[(j - 1) if up else (j + 1) % NZ, h]
+        where = self.at(0, 1) if up else self.at(0, NZ - 1)
+        return self.remote(src, self.G.at[j, h], self.gsend.at[j, h], self.grecv.at[j, h], where)
+
+    def code(self, j):
+        return self.remote(self.C.at[0], self.C.at[j], self.csend.at[j], self.crecv.at[j], self.at(0, j))
+
+    def bucket(self, ph, j, kind):
+        into, through = (self.A, self.TA) if ph == 0 else (self.B, self.TB)
+
+        def lead(i):
+            return into.at[i, j] if ph == 0 else into.at[j, i]
+
+        send, recv = self.xsend.at[ph, j, kind], self.xrecv.at[ph, j, kind]
+        up, down = self.at(1, 0), self.at(NX - 1, 0)
+        if kind == 0:
+            return self.remote(self.Q.at[ph, j, 0], lead(3), send, recv, up)
+        if kind == 1:
+            return self.remote(self.Q.at[ph, j, 1], lead(1), send, recv, down)
+        h = kind % 2
+        where = down if h else up
+        if kind < 4:
+            return self.remote(self.QH.at[ph, j, h], through.at[j, h], send, recv, where)
+        dst = lead(2).at[:, self.cols(h)]
+        return self.remote(through.at[j, h], dst, send, recv, where)
+
+    def send_buckets(self, ph, j, rows):
+        n = BUCKET
+        for h in range(2):
+            self.QH[ph, j, h] = rows[2 * n : 3 * n, h * self.half : (h + 1) * self.half]
+            self.bucket(ph, j, 2 + h).start()
+        self.Q[ph, j, 0] = rows[n : 2 * n]
+        self.bucket(ph, j, 0).start()
+        self.Q[ph, j, 1] = rows[3 * n :]
+        self.bucket(ph, j, 1).start()
+        if ph == 0:
+            self.A[0, j] = rows[:n]
+        else:
+            self.B[j, 0] = rows[:n]
+
+    def relay(self, ph, j):
+        for h in range(2):
+            self.bucket(ph, j, 2 + h).wait_recv()
+            self.bucket(ph, j, 4 + h).start()
+
+    def wait_buckets(self, ph, j):
+        for kind in (0, 1, 4, 5):
+            self.bucket(ph, j, kind).wait_recv()
+
+    def row_codes(self, shape, dim):
+        line = lax.broadcasted_iota(jnp.int32, shape, dim)
+        dx = sum((line >= BUCKET * k).astype(jnp.int32) for k in (1, 2, 3))
+        rank = line - BUCKET * dx
+        owner = ((self.x + dx) % NX) * NZ + self.z
+        return jnp.where(line < BUCKET * NX, owner * BUCKET + rank, -7)
+
+    def select(self, j):
+        rows = self.row_codes((NX * BUCKET, self.C.shape[2]), 0)
+        hit = (rows == self.C[j, 0:1]) | (rows == self.C[j, 1:2])
+        hit = hit.astype(F32).astype(BF16)
+        left, right = dot(hit, self.G[j, 0]), dot(hit, self.G[j, 1])
+        self.send_buckets(0, j, jnp.concatenate([left, right], axis=1).astype(BF16))
+
+    def dispatch(self, tokens, gain, pos, rows):
+        values = tokens[...].astype(F32)
+        scale = lax.rsqrt(jnp.mean(values * values, axis=-1, keepdims=True) + EPSILON)
+        normed = (values * scale * gain[...]).astype(BF16)
+        for h in range(2):
+            self.G[0, h] = normed[:, h * self.half : (h + 1) * self.half]
+            self.spread(1, h, True).start()
+            self.spread(NZ - 1, h, False).start()
+        for j in range(1, NZ):
+            self.code(j).start()
+        self.select(0)
+        for s in (1, 2, 3):
+            for h in range(2):
+                self.spread(s, h, True).wait_recv()
+                if s < 3 or h == 0:
+                    self.spread(s + 1, h, True).start()
+                self.spread(NZ - s, h, False).wait_recv()
+                if s < 3 or h == 1:
+                    self.spread(NZ - s - 1, h, False).start()
+            for j in (0,) if s == 1 else (s - 1, NZ - s + 1):
+                self.relay(0, j)
+            for j in (s, NZ - s):
+                self.code(j).wait_recv()
+                self.select(j)
+        self.code(4).wait_recv()
+        self.spread(4, 0, True).wait_recv()
+        self.spread(4, 1, False).wait_recv()
+        self.select(4)
+        for j in (3, 5, 4):
+            self.relay(0, j)
+        experts, cap, width = rows.shape
+        blocks = []
+        for b in range(2):
+            places = lane_rows(pos[0:1, b * 128 : (b + 1) * 128], 128)[:, :1]
+            blocks.append(places)
+        for j in range(NZ):
+            self.wait_buckets(0, j)
+        count = NX * NZ * BUCKET
+        arrived = self.A[...].reshape(count, width)
+        for b, places in enumerate(blocks):
+            hit = (places == lax.broadcasted_iota(jnp.int32, (128, count), 1)).astype(F32).astype(BF16)
+            got = dot(hit, arrived).astype(BF16)
+            per = 128 // cap
+            for i in range(per):
+                rows[b * per + i] = got[i * cap : (i + 1) * cap]
+
+    def expanders(self):
+        codes = self.row_codes((128, 128), 1)
+        for j in range(NZ):
+            first, second = lane_rows(self.C[j, 0:1], 128), lane_rows(self.C[j, 1:2], 128)
+            self.OT[j] = ((first == codes) | (second == codes)).astype(F32).astype(BF16)
+
+    def give_back(self, tokens, pos, weighted, out):
+        experts, cap, width = weighted.shape
+        slots = experts * cap
+        n = NX * BUCKET
+        line = lax.broadcasted_iota(jnp.int32, (n, slots), 0)
+        dx = sum((line >= BUCKET * k).astype(jnp.int32) for k in (1, 2, 3))
+        base = dx * (NZ * BUCKET) + (line - BUCKET * dx)
+
+        def send(j):
+            hit = (base + j * BUCKET == pos[0:1, :]).astype(F32).astype(BF16)
+            self.send_buckets(1, j, dot(hit, weighted[...].reshape(slots, width)).astype(BF16))
+
+        def landed(j):
+            self.wait_buckets(1, j)
+
+        def part(j, h):
+            rows = self.B[j, :, :, h * self.half : (h + 1) * self.half].reshape(n, self.half)
+            return dot(self.OT[j][:, :n], rows)
+
+        def fold(j, h, up):
+            where, way = (self.at(0, 1), 0) if up else (self.at(0, NZ - 1), 1)
+            there = (j + 1) % NZ if up else j - 1
+            return self.remote(
+                self.V.at[j, h], self.RP.at[way, there, h],
+                self.vsend.at[j, h], self.vrecv.at[way, there, h], where,
+            )
+
+        def got(j, h, up):
+            fold((j - 1) % NZ if up else j + 1, h, up).wait_recv()
+            return self.RP[0 if up else 1, j, h].astype(F32)
+
+        def emit(j, h, up, incoming):
+            value = part(j, h)
+            if incoming:
+                value = value + got(j, h, up)
+            self.V[j, h] = value.astype(BF16)
+            fold(j, h, up).start()
+
+        send(4)
+        send(5)
+        send(3)
+        self.relay(1, 4)
+        landed(4)
+        emit(4, 0, True, False)
+        emit(4, 1, False, False)
+        for s, ahead in ((1, (6, 2)), (2, (7, 1)), (3, (0,))):
+            for j in ahead:
+                send(j)
+            up, down = 4 + s, 4 - s
+            for j in (up, down):
+                self.relay(1, j)
+            for j in (up, down):
+                landed(j)
+            emit(up, 1, True, s > 1)
+            emit(down, 0, False, s > 1)
+            emit(up, 0, True, True)
+            emit(down, 1, False, True)
+        self.relay(1, 0)
+        landed(0)
+        for h in (1, 0):
+            cut = slice(h * self.half, (h + 1) * self.half)
+            total = tokens[:, cut].astype(F32) + part(0, h)
+            total = total + got(0, h, True) + got(0, h, False)
+            out[:, cut] = total.astype(BF16)
+        for ph in range(2):
+            for j in range(NZ):
+                for kind in range(6):
+                    self.bucket(ph, j, kind).wait_send()
+        for j in range(1, NZ):
+            self.code(j).wait_send()
+            for h in range(2):
+                up = j < 4 or (j == 4 and h == 0)
+                self.spread(j, h, up).wait_send()
+                fold(j, h, j > 4 or (j == 4 and h == 0)).wait_send()
+
+
+def exchange_scratch(tok_rows, width):
+    dma = pltpu.SemaphoreType.DMA
+    half = width // 2
+    return dict(
+        G=pltpu.VMEM((NZ, 2, tok_rows, half), BF16),
+        C=pltpu.VMEM((NZ, 8, tok_rows), jnp.int32),
+        Q=pltpu.VMEM((2, NZ, 2, BUCKET, width), BF16),
+        QH=pltpu.VMEM((2, NZ, 2, BUCKET, half), BF16),
+        A=pltpu.VMEM((NX, NZ, BUCKET, width), BF16),
+        B=pltpu.VMEM((NZ, NX, BUCKET, width), BF16),
+        TA=pltpu.VMEM((NZ, 2, BUCKET, half), BF16),
+        TB=pltpu.VMEM((NZ, 2, BUCKET, half), BF16),
+        OT=pltpu.VMEM((NZ, 128, 128), BF16),
+        V=pltpu.VMEM((NZ, 2, tok_rows, half), BF16),
+        RP=pltpu.VMEM((2, NZ, 2, tok_rows, half), BF16),
+        gsend=dma((NZ, 2)),
+        grecv=dma((NZ, 2)),
+        csend=dma((NZ,)),
+        crecv=dma((NZ,)),
+        xsend=dma((2, NZ, 6)),
+        xrecv=dma((2, NZ, 6)),
+        vsend=dma((NZ, 2)),
+        vrecv=dma((2, NZ, 2)),
+    )
+
+
+def expert_layer(
+    rows, router, w1_hbm, w2_hbm, out, meanwhile,
     X, W1, W2, PS, R, S, T, F,
     w_sem, sendP, recvP, sendI, recvI, rsend, rrecv, fsend, frecv, tsend, trecv,
 ):
@@ -47,18 +277,6 @@
     minus = ((y + 3) % 4) * 2 + c
     half = experts // 2
 
-    weights = []
-    for e in range(experts):
-        weights.append(pltpu.make_async_copy(w1_hbm.at[e], W1.at[e], w_sem.at[0, e]))
-        weights.append(pltpu.make_async_copy(w2_hbm.at[e], W2.at[e], w_sem.at[1, e]))
-    for copy in weights:
-        copy.start()
-
-    barrier = pltpu.get_barrier_semaphore()
-    for other in (partner, plus, minus):
-        pl.semaphore_signal(barrier, inc=1, device_id={"dat": other}, device_id_type=MESH)
-    pl.semaphore_wait(barrier, 3)
-
     def remote(src, dst, send, recv, where):
         return pltpu.make_async_remote_copy(
             src_ref=src, dst_ref=dst, send_sem=send, recv_sem=recv, device_id={"dat": where}, device_id_type=MESH
@@ -111,6 +329,7 @@
         to_partner(0, k).start()
     for e in range(experts):
         X[0, e, :C] = rows[e]
+    meanwhile()
 
     def first(e, carry):
         remote(rows.at[e], X.at[0, e, other_rows], sendP.at[0, e], recvP.at[0, e], partner).wait_recv()
@@ -197,83 +416,104 @@
             part_to_partner(s, e).wait_send()
 
 
-def expert_layer(rows, router, inner_weight, outer_weight):
-    experts, C, width = rows.shape
-    hidden = inner_weight.shape[2]
+def expert_scratch(experts, C, width, hidden):
     dma = pltpu.SemaphoreType.DMA
+    return dict(
+        X=pltpu.VMEM((4, experts, 2 * C, width), BF16),
+        W1=pltpu.VMEM((experts, width, hidden), BF16),
+        W2=pltpu.VMEM((experts, hidden, width), BF16),
+        PS=pltpu.VMEM((4, experts, 2 * C, width), BF16),
+        R=pltpu.VMEM((4, experts, C, width), BF16),
+        S=pltpu.VMEM((4, experts, C, width), BF16),
+        T=pltpu.VMEM((experts, C, width), BF16),
+        F=pltpu.VMEM((2, experts, C, width), BF16),
+        w_sem=dma((2, experts)),
+        sendP=dma((4, experts)),
+        recvP=dma((4, experts)),
+        sendI=dma((4, experts)),
+        recvI=dma((4, experts)),
+        rsend=dma((4, experts)),
+        rrecv=dma((4, experts)),
+        fsend=dma((2, experts)),
+        frecv=dma((2, experts)),
+        tsend=dma((experts,)),
+        trecv=dma((experts,)),
+    )
+
+
+def layer_kernel(names, with_experts, tokens, gain, codes, pos, router, w1_hbm, w2_hbm, out, rows, weighted, *refs):
+    refs = dict(zip(names, refs))
+    width = tokens.shape[1]
+    experts = rows.shape[0]
+    mine = {k: refs.pop(k) for k in exchange_scratch(8, 8)}
+    exchange = Exchange(mine, width)
+    if with_experts:
+        for e in range(experts):
+            pltpu.make_async_copy(w1_hbm.at[e], refs["W1"].at[e], refs["w_sem"].at[0, e]).start()
+            pltpu.make_async_copy(w2_hbm.at[e], refs["W2"].at[e], refs["w_sem"].at[1, e]).start()
+    dat = lax.axis_index("dat")
+    c, y = dat % 2, dat // 2
+    barrier = pltpu.get_barrier_semaphore()
+    others = [{"exp": where} for where in exchange.peers()]
+    if with_experts:
+        others += [{"dat": y * 2 + 1 - c}, {"dat": ((y + 1) % 4) * 2 + c}, {"dat": ((y + 3) % 4) * 2 + c}]
+    for other in others:
+        pl.semaphore_signal(barrier, inc=1, device_id=other, device_id_type=MESH)
+    exchange.C[0] = codes[...]
+    pl.semaphore_wait(barrier, len(others))
+    exchange.dispatch(tokens, gain, pos, rows)
+    if with_experts:
+        expert_layer(rows, router, w1_hbm, w2_hbm, weighted, exchange.expanders, **refs)
+    else:
+        exchange.expanders()
+        for e in range(experts):
+            weighted[e] = rows[e]
+    exchange.give_back(tokens, pos, weighted, out)
+
+
+def whole_layer(tokens, gain, codes, pos, router, inner_weight, outer_weight, with_experts=True):
+    tok_rows, width = tokens.shape
+    experts, _, hidden = inner_weight.shape
+    cap = pos.shape[1] // experts
     vmem = pl.BlockSpec(memory_space=pltpu.VMEM)
     hbm = pl.BlockSpec(memory_space=pl.ANY)
+    scratch = exchange_scratch(tok_rows, width)
+    if with_experts:
+        scratch.update(expert_scratch(experts, cap, width, hidden))
+    slots = pltpu.VMEM((experts, cap, width), BF16)
     return pl.pallas_call(
-        ffn_kernel,
-        name="expert_layer",
-        out_shape=jax.ShapeDtypeStruct((experts, C, width), BF16),
-        in_specs=[vmem, vmem, hbm, hbm],
+        functools.partial(layer_kernel, tuple(scratch), with_experts),
+        name="whole_layer",
+        out_shape=jax.ShapeDtypeStruct((tok_rows, width), BF16),
+        in_specs=[vmem] * 5 + [hbm] * 2,
         out_specs=vmem,
-        scratch_shapes=[
-            pltpu.VMEM((4, experts, 2 * C, width), BF16),
-            pltpu.VMEM((experts, width, hidden), BF16),
-            pltpu.VMEM((experts, hidden, width), BF16),
-            pltpu.VMEM((4, experts, 2 * C, width), BF16),
-            pltpu.VMEM((4, experts, C, width), BF16),
-            pltpu.VMEM((4, experts, C, width), BF16),
-            pltpu.VMEM((experts, C, width), BF16),
-            pltpu.VMEM((2, experts, C, width), BF16),
-            dma((2, experts)),
-            dma((4, experts)),
-            dma((4, experts)),
-            dma((4, experts)),
-            dma((4, experts)),
-            dma((4, experts)),
-            dma((4, experts)),
-            dma((2, experts)),
-            dma((2, experts)),
-            dma((experts,)),
-            dma((experts,)),
-        ],
+        scratch_shapes=[slots, slots] + list(scratch.values()),
         compiler_params=pltpu.CompilerParams(
             collective_id=0, has_side_effects=True, vmem_limit_bytes=60 * 1024 * 1024
         ),
-    )(rows, router, inner_weight, outer_weight)
+    )(tokens, gain, codes, pos, router, inner_weight, outer_weight)
+
+
+def routes(slot_tokens, slot_ids, tok_rows, dat_count):
+    experts_dev, cap_dev = slot_tokens.shape
+    x, z = lax.axis_index("exp") // NZ, lax.axis_index("exp") % NZ
+    flat_ids = slot_ids.T.reshape(-1)
+    owner = flat_ids // (experts_dev * cap_dev * dat_count)
+    before = (owner[:, None] == owner[None, :]) & (flat_ids[:, None] < flat_ids[None, :])
+    codes = owner * BUCKET + jnp.sum(before.astype(jnp.int32), axis=0)
+    codes = jnp.pad(codes.reshape(2, tok_rows), ((0, 6), (0, 0)), constant_values=-1)
+    picked = slot_tokens.reshape(-1)
+    keys = lax.iota(jnp.int32, experts_dev * cap_dev)
+    source = picked // (tok_rows * dat_count)
+    before = (source[:, None] == source[None, :]) & (keys[:, None] < keys[None, :])
+    rank = jnp.sum(before.astype(jnp.int32), axis=0)
+    place = ((source // NZ - x) % NX) * NZ + (z - source % NZ) % NZ
+    return codes, (place * BUCKET + rank)[None, :]
 
 
 def body(tokens, norm_gain, router_weight, inner_weight, outer_weight, slot_tokens, slot_ids):
-    exp_count = lax.axis_size("exp")
-    dat_count = lax.axis_size("dat")
-    tok_rows, width = tokens.shape
-    experts_dev, cap_dev = slot_tokens.shape
-    bucket = 6 * tok_rows // exp_count
-    normed = normalize(tokens, norm_gain)
-    picked = slot_tokens.reshape(-1)
-    slot_keys = lax.iota(jnp.int32, experts_dev * cap_dev)
-    senders = expert_places(picked, slot_keys, tok_rows, dat_count, bucket)
-    receivers = owner_places(slot_ids, experts_dev, cap_dev * dat_count, bucket)
-    lookup = jnp.any(
-        lax.broadcasted_iota(jnp.int32, (exp_count * bucket, 1, 1), 0) == receivers[None], axis=2
-    )
-    outgoing = jnp.dot(lookup.astype(BF16), normed, preferred_element_type=F32)
-    outgoing = outgoing.astype(BF16).reshape(exp_count, bucket, width)
-    arrived = lax.all_to_all(outgoing, "exp", split_axis=0, concat_axis=0, tiled=True).reshape(
-        exp_count * bucket, width
-    )
-    placing = lax.broadcasted_iota(jnp.int32, (exp_count * bucket, 1), 0) == senders[None, :]
-    placing = placing.astype(BF16)
-    gathered_rows = lax.dot_general(
-        placing, arrived, (((0,), (0,)), ((), ())), preferred_element_type=F32
-    ).astype(BF16)
-    gathered_rows = gathered_rows.reshape(experts_dev, cap_dev, width)
-    weighted = expert_layer(gathered_rows, router_weight.T, inner_weight, outer_weight)
-    weighted = weighted.reshape(-1, width)
-    returning = jnp.dot(placing, weighted, preferred_element_type=F32)
-    returning = returning.astype(BF16).reshape(exp_count, bucket, width)
-    came_back = lax.all_to_all(returning, "exp", split_axis=0, concat_axis=0, tiled=True).reshape(
-        exp_count * bucket, width
-    )
-    combine_table = jnp.sum(
-        (lax.broadcasted_iota(jnp.int32, (1, 1, exp_count * bucket), 2) == receivers[:, :, None]).astype(F32),
-        axis=1,
-    )
-    combined = jnp.dot(combine_table.astype(BF16), came_back, preferred_element_type=F32)
-    return (tokens.astype(F32) + combined).astype(BF16)
+    codes, pos = routes(slot_tokens, slot_ids, tokens.shape[0], lax.axis_size("dat"))
+    return whole_layer(tokens, norm_gain[None, :], codes, pos, router_weight.T, inner_weight, outer_weight)
 
 
 def solution(mesh):

time: 150 us -> 123 us (0.82); the launches traced: 147 us -> 122 us
  waiting for transfers between devices: 77.3 us -> 0 us
  Pallas kernels: 40.5 us -> 116 us
  starting transfers between devices: 17.4 us -> 0 us
  matrix products: 8.03 us -> 0 us
  local copies, waits for them, and re-layouts: 1.21 us -> 3.8 us
    all_to_all x2 -> x0, waiting for transfers between devices: 77.3 us -> none  [the longest x1 39 us: body(): lax.all_to_all(outgoing, 'exp', split_axis=0, concat_axis=0, tiled=True)]
    pallas_call x1, Pallas kernels: 40.5 us -> 116 us  [whole_layer(): pl.pallas_call(functools.partial(layer_kernel, tuple(scratch), with_exper...]
    all_to_all x2 -> x0, starting transfers between devices: 17.4 us -> none  [the longest x1 11.4 us: body(): lax.all_to_all(outgoing, 'exp', split_axis=0, concat_axis=0, tiled=True)]
    dot_general x4 -> x0, matrix products: 8.03 us -> none  [the longest x1 2.78 us: body(): returning = jnp.dot(placing, weighted, preferred_element_type=F32)]
  transfers between devices with their start and end apart: 2 -> 0, of which waited for: 2 -> 0; matrix products, arithmetic and copies ran while one was open for 0% -> 0% of each run, Pallas kernels for 0% -> 0%
where the time goes in v2:
time: 123 us; the launch traced here: 122 us
  Pallas kernels  116 us (94%)
  local copies, waits for them, and re-layouts  3.8 us (3%)
  other arithmetic  3.01 us (2%)
    pallas_call x1, Pallas kernels, whole_layer(): pl.pallas_call(functools.partial(layer_kernel, tuple(scratch), with_exper...  116 us

profile of v2, /device:TPU:8, one launch (start us, length us, event | category | flops | bytes accessed | tf_op | source)
XLA Modules:
  0.0 122.3 jit_solution(14801078290745629937)
XLA Ops:
  0.0 0.8 reshape.329
  0.8 0.1 convert_reduce_fusion
  0.9 0.8 reshape.328
  1.7 0.6 multiply_add_fusion.pos
  2.3 0.7 and_select_fusion.6
  2.9 0.9 convert_reduce_fusion.1
  3.8 0.7 bitcast_add_fusion
  4.5 0.6 pad.4.codes
  5.1 115.5 %whole_layer.1 = bf16[128,1024]{1,0:T(8,128)(2,1)} custom-call(bf16[128,1024]{1,0:T(8,128)(2,1)} %tokens.1, f32[1,1024]{1,0:T(1,128)} %bitcast.20, s32[8,128]{1,0:T(8,128)} %pad.4.codes, s32[1,256]{1,0:T(1,128)} %multiply_add_fusion.pos, bf16[4,1024]{1,0:T(4,128)(2,1)} %bitcast.19, bf16[4,1024,512]{2,1,0:T(8,128)(2,1)} %w1_hbm.1, bf16[4,512,1024]{2,1,0:T(8,128)(2,1)} %w2_hbm.1), custom_call_target="tpu_custom_call" | custom-call | tf_op jit(solution)/shard_map/whole_layer/pallas_call | solution.py:484
  120.7 1.7 %copy.9 = bf16[128,1024]{1,0:T(8,128)(2,1)} copy(bf16[128,1024]{1,0:T(8,128)(2,1)} %whole_layer.1) | data formatting | bytes 524288
  (1 shorter events, 0.0 us)

commit v3 on v0

v3 whole, which is shorter than its diff:
```python
import functools

import jax
import jax.numpy as jnp
from jax import lax
from jax.experimental import pallas as pl
from jax.experimental.pallas import tpu as pltpu
from jax.sharding import PartitionSpec as P

EPSILON = 1e-06
MESH = pl.DeviceIdType.MESH
BF16 = jnp.bfloat16
F32 = jnp.float32
I32 = jnp.int32

NX, NZ, NY = 4, 8, 4
BUCKET = 24
FAR = NZ // 2


def dot(a, b):
    return jnp.dot(a, b, preferred_element_type=F32)


def onehot(mask):
    return mask.astype(F32).astype(BF16)


def down_rows(row):
    n = row.shape[1]
    return jnp.transpose(jnp.broadcast_to(row, (n, n)))


def count(mask):
    return jnp.sum(mask.astype(F32), axis=0, keepdims=True).astype(I32)


def remote(src, dst, send, recv, where):
    return pltpu.make_async_remote_copy(
        src_ref=src, dst_ref=dst, send_sem=send, recv_sem=recv, device_id=where, device_id_type=MESH
    )


class Exchange:
    def __init__(self, refs, width):
        self.__dict__.update(refs)
        exp = lax.axis_index("exp")
        self.x, self.z = exp // NZ, exp % NZ
        self.chunk, self.piece = width // 2, width // 4

    def at(self, dx, dz):
        return {"exp": ((self.x + dx) % NX) * NZ + (self.z + dz) % NZ}

    def peers(self):
        return [self.at(0, 1), self.at(0, NZ - 1)] + [self.at(dx, 0) for dx in range(1, NX)]

    def routes(self, slot_ids, slot_tokens, tok_rows, slots, dat_count):
        ids = [slot_ids[k : k + 1] for k in range(2)]
        owners = [row // (slots * dat_count) for row in ids]
        for k in range(2):
            rank = 0
            for m in range(2):
                rank = rank + count((down_rows(owners[m]) == owners[k]) & (down_rows(ids[m]) < ids[k]))
            self.C[0, k : k + 1] = owners[k] * BUCKET + rank
        experts = slot_tokens.shape[0]
        per = experts // 2
        source = [
            jnp.concatenate([slot_tokens[b * per + i : b * per + i + 1] for i in range(per)], axis=1)
            // (tok_rows * dat_count)
            for b in range(2)
        ]
        n = slots // 2
        earlier = lax.broadcasted_iota(I32, (n, n), 0) < lax.broadcasted_iota(I32, (n, n), 1)
        for b in range(2):
            rank = count((down_rows(source[b]) == source[b]) & earlier)
            if b == 1:
                rank = rank + count(down_rows(source[0]) == source[1])
            place = ((source[b] // NZ - self.x + NX) % NX) * NZ + (self.z - source[b] % NZ + NZ) % NZ
            self.PO[b : b + 1] = place * BUCKET + rank

    def spread(self, j, p, up):
        src = self.G.at[(j - 1) if up else (j + 1) % NZ, p]
        where = self.at(0, 1) if up else self.at(0, NZ - 1)
        return remote(src, self.G.at[j, p], self.gsend.at[j, p], self.grecv.at[j, p], where)

    def code(self, j):
        up = j <= FAR
        src = self.C.at[(j - 1) if up else (j + 1) % NZ]
        where = self.at(0, 1) if up else self.at(0, NZ - 1)
        return remote(src, self.C.at[j], self.csend.at[j], self.crecv.at[j], where)

    def open_codes(self):
        self.code(1).start()
        self.code(NZ - 1).start()

    def code_hop(self, s):
        self.code(s).wait_recv()
        if s < FAR:
            self.code(s + 1).start()
            self.code(NZ - s).wait_recv()
            if s < FAR - 1:
                self.code(NZ - s - 1).start()

    def bucket(self, ph, q, j, kind):
        def place(i):
            return self.A.at[q, i, j] if ph == 0 else self.B.at[q, j, i]

        send, recv = self.xsend.at[ph, q, j, kind], self.xrecv.at[ph, q, j, kind]
        up, down = self.at(1, 0), self.at(NX - 1, 0)
        if kind == 0:
            return remote(self.Q.at[ph, q, j, 0], place(3), send, recv, up)
        if kind == 1:
            return remote(self.Q.at[ph, q, j, 1], place(1), send, recv, down)
        h = kind % 2
        half = place(2).at[:, pl.ds(h * self.piece, self.piece)]
        where = down if h else up
        if kind >= 4:
            return remote(self.TR.at[ph, q, j, h], half, send, recv, where)
        if j == FAR:
            return remote(self.QH.at[ph, q, j, h], half, send, recv, self.at(2, 0))
        return remote(self.QH.at[ph, q, j, h], self.TR.at[ph, q, j, h], send, recv, where)

    def send_buckets(self, ph, q, j, rows):
        n = BUCKET
        for h in range(2):
            self.QH[ph, q, j, h] = rows[2 * n : 3 * n, h * self.piece : (h + 1) * self.piece]
            self.bucket(ph, q, j, 2 + h).start()
        self.Q[ph, q, j, 0] = rows[n : 2 * n]
        self.bucket(ph, q, j, 0).start()
        self.Q[ph, q, j, 1] = rows[3 * n :]
        self.bucket(ph, q, j, 1).start()
        if ph == 0:
            self.A[q, 0, j] = rows[:n]
        else:
            self.B[q, j, 0] = rows[:n]

    def relay(self, ph, q, *js):
        for j in js:
            if j != FAR:
                for h in range(2):
                    self.bucket(ph, q, j, 2 + h).wait_recv()
                    self.bucket(ph, q, j, 4 + h).start()

    def landed(self, ph, q, j):
        for kind in (0, 1, 2, 3) if j == FAR else (0, 1, 4, 5):
            self.bucket(ph, q, j, kind).wait_recv()

    def row_codes(self, shape, dim):
        line = lax.broadcasted_iota(I32, shape, dim)
        dx = sum((line >= BUCKET * k).astype(I32) for k in (1, 2, 3))
        owner = ((self.x + dx) % NX) * NZ + self.z
        return jnp.where(line < BUCKET * NX, owner * BUCKET + line - BUCKET * dx, -7)

    def select(self, q, *js):
        for j in js:
            rows = self.row_codes((NX * BUCKET, self.C.shape[2]), 0)
            hit = onehot((rows == self.C[j, 0:1]) | (rows == self.C[j, 1:2]))
            parts = [dot(hit, self.G[j, 2 * q + h]) for h in range(2)]
            self.send_buckets(0, q, j, jnp.concatenate(parts, axis=1).astype(BF16))

    def normalize(self, tokens, gain):
        values = tokens[...].astype(F32)
        scale = lax.rsqrt(jnp.mean(values * values, axis=-1, keepdims=True) + EPSILON)
        normed = (values * scale * gain[...]).astype(BF16)
        for p in range(4):
            self.G[0, p] = normed[:, p * self.piece : (p + 1) * self.piece]

    def open_ring(self, *ps):
        for p in ps:
            self.spread(1, p, True).start()
            self.spread(NZ - 1, p, False).start()

    def hop(self, s, *ps):
        for p in ps:
            for up in (True, False):
                j, onward = (s, s + 1) if up else (NZ - s, NZ - s - 1)
                far_way = up == (p % 2 == 0)
                if s < FAR or far_way:
                    self.spread(j, p, up).wait_recv()
                if s < FAR - 1 or (s == FAR - 1 and far_way):
                    self.spread(onward, p, up).start()

    def compact(self, q, rows):
        for j in range(NZ):
            self.landed(0, q, j)
        _, experts, cap, width = rows.shape
        total = NX * NZ * BUCKET
        arrived = self.A[q].reshape(total, width)
        per = experts // 2
        for b in range(2):
            places = down_rows(self.PO[b : b + 1])[:, :1]
            hit = onehot(places == lax.broadcasted_iota(I32, (per * cap, total), 1))
            got = dot(hit, arrived).astype(BF16)
            for i in range(per):
                rows[q, b * per + i] = got[i * cap : (i + 1) * cap]

    def expanders(self):
        n = self.C.shape[2]
        codes = self.row_codes((n, 128), 1)
        for j in range(NZ):
            first, second = down_rows(self.C[j, 0:1]), down_rows(self.C[j, 1:2])
            self.OT[j] = onehot((first == codes) | (second == codes))

    def send_back(self, q, weighted, *js):
        _, experts, cap, width = weighted.shape
        per = experts // 2
        line = lax.broadcasted_iota(I32, (NX * BUCKET, per * cap), 0)
        dx = sum((line >= BUCKET * k).astype(I32) for k in (1, 2, 3))
        base = dx * (NZ * BUCKET) + line - BUCKET * dx
        for j in js:
            out = 0
            for b in range(2):
                hit = onehot(base + j * BUCKET == self.PO[b : b + 1])
                out = out + dot(hit, weighted[q, b * per : (b + 1) * per].reshape(per * cap, width))
            self.send_buckets(1, q, j, out.astype(BF16))

    def part(self, j, p):
        q, h = p // 2, p % 2
        n = NX * BUCKET
        rows = self.B[q, j, :, :, h * self.piece : (h + 1) * self.piece].reshape(n, self.piece)
        return dot(self.OT[j][:, :n], rows)

    def fold(self, j, p, up):
        where, way = (self.at(0, 1), 0) if up else (self.at(0, NZ - 1), 1)
        there = (j + 1) % NZ if up else j - 1
        return remote(
            self.V.at[j, p], self.RP.at[way, there, p], self.vsend.at[j, p], self.vrecv.at[way, there, p], where
        )

    def carried(self, j, p, up):
        self.fold((j - 1) % NZ if up else j + 1, p, up).wait_recv()
        return self.RP[0 if up else 1, j, p].astype(F32)

    def emit(self, j, p, up, incoming):
        value = self.part(j, p)
        if incoming:
            value = value + self.carried(j, p, up)
        self.V[j, p] = value.astype(BF16)
        self.fold(j, p, up).start()

    def fold_far(self, q):
        self.landed(1, q, FAR)
        self.emit(FAR, 2 * q, True, False)
        self.emit(FAR, 2 * q + 1, False, False)

    def fold_step(self, q, s):
        up, down = FAR + s, FAR - s
        even, odd = 2 * q, 2 * q + 1
        for j in (up, down):
            self.landed(1, q, j)
        self.emit(up, odd, True, s > 1)
        self.emit(down, even, False, s > 1)
        self.emit(up, even, True, True)
        self.emit(down, odd, False, True)

    def fold_end(self, q, tokens, out):
        self.landed(1, q, 0)
        for p in (2 * q, 2 * q + 1):
            cut = slice(p * self.piece, (p + 1) * self.piece)
            total = tokens[:, cut].astype(F32) + self.part(0, p)
            total = total + self.carried(0, p, True) + self.carried(0, p, False)
            out[:, cut] = total.astype(BF16)

    def drain(self, ph):
        for q in range(2):
            for j in range(NZ):
                for kind in range(4 if j == FAR else 6):
                    self.bucket(ph, q, j, kind).wait_send()
        for j in range(1, NZ):
            if ph == 0:
                self.code(j).wait_send()
            for p in range(4):
                far_up = j == FAR and p % 2 == 0
                if ph == 0:
                    self.spread(j, p, j < FAR or far_up).wait_send()
                else:
                    self.fold(j, p, j > FAR or far_up).wait_send()

    @staticmethod
    def scratch(tok_rows, width, slots):
        dma = pltpu.SemaphoreType.DMA
        chunk, piece = width // 2, width // 4
        return dict(
            G=pltpu.VMEM((NZ, 4, tok_rows, piece), BF16),
            C=pltpu.VMEM((NZ, 2, tok_rows), I32),
            PO=pltpu.VMEM((2, slots // 2), I32),
            Q=pltpu.VMEM((2, 2, NZ, 2, BUCKET, chunk), BF16),
            QH=pltpu.VMEM((2, 2, NZ, 2, BUCKET, piece), BF16),
            TR=pltpu.VMEM((2, 2, NZ, 2, BUCKET, piece), BF16),
            A=pltpu.VMEM((2, NX, NZ, BUCKET, chunk), BF16),
            B=pltpu.VMEM((2, NZ, NX, BUCKET, chunk), BF16),
            OT=pltpu.VMEM((NZ, tok_rows, 128), BF16),
            V=pltpu.VMEM((NZ, 4, tok_rows, piece), BF16),
            RP=pltpu.VMEM((2, NZ, 4, tok_rows, piece), BF16),
            gsend=dma((NZ, 4)),
            grecv=dma((NZ, 4)),
            csend=dma((NZ,)),
            crecv=dma((NZ,)),
            xsend=dma((2, 2, NZ, 6)),
            xrecv=dma((2, 2, NZ, 6)),
            vsend=dma((NZ, 4)),
            vrecv=dma((2, NZ, 4)),
        )


class Experts:
    def __init__(self, refs, rows, router, w1_hbm, w2_hbm):
        self.__dict__.update(refs)
        self.rows, self.router, self.w1_hbm, self.w2_hbm = rows, router, w1_hbm, w2_hbm
        _, self.experts, self.cap, self.chunk = rows.shape
        self.half = self.experts // 2
        dat = lax.axis_index("dat")
        c, y = dat % 2, dat // 2
        self.partner = {"dat": y * 2 + 1 - c}
        self.plus = {"dat": ((y + 1) % NY) * 2 + c}
        self.minus = {"dat": ((y + NY - 1) % NY) * 2 + c}
        self.own, self.other = pl.ds(0, self.cap), pl.ds(self.cap, self.cap)

    def peers(self):
        return [self.partner, self.plus, self.minus]

    def weights(self, e):
        return [
            pltpu.make_async_copy(self.w1_hbm.at[e], self.W1.at[e], self.w_sem.at[0, e]),
            pltpu.make_async_copy(self.w2_hbm.at[e], self.W2.at[e], self.w_sem.at[1, e]),
        ]

    def load(self):
        for e in range(self.experts):
            for copy in self.weights(e):
                copy.start()

    def direct(self, q, s, e):
        return remote(
            self.rows.at[q, e], self.X.at[q, e, s, self.own], self.sendI.at[q, s, e], self.recvI.at[q, s, e],
            self.plus if s == 1 else self.minus,
        )

    def onward(self, q, e):
        s, where = (1, self.plus) if e < self.half else (2, self.minus)
        return remote(
            self.X.at[q, e, s, self.own], self.X.at[q, e, 3, self.own],
            self.sendI.at[q, 3, e], self.recvI.at[q, 3, e], where,
        )

    def across(self, q, s, e, own=False):
        src = self.rows.at[q, e] if own else self.X.at[q, e, s, self.own]
        return remote(
            src, self.X.at[q, e, s, self.other], self.sendP.at[q, s, e], self.recvP.at[q, s, e], self.partner
        )

    def part_across(self, q, s, e):
        return remote(
            self.PS.at[q, e, s, self.other], self.R.at[q, e, s],
            self.rsend.at[q, s, e], self.rrecv.at[q, s, e], self.partner,
        )

    def final(self, q, up, e):
        src, i, where = (self.S.at[q, e, 2], 0, self.plus) if up else (self.S.at[q, e, 1], 1, self.minus)
        return remote(src, self.F.at[q, i, e], self.fsend.at[q, i, e], self.frecv.at[q, i, e], where)

    def transit(self, q, e):
        where = self.plus if e < self.half else self.minus
        return remote(self.S.at[q, e, 3], self.T.at[q, e], self.tsend.at[q, e], self.trecv.at[q, e], where)

    def pairs(self, k):
        experts, half = self.experts, self.half
        if k < experts:
            return [(1, k), (2, (k + half) % experts)]
        if k < experts + half:
            return [(3, k - experts), (3, k - experts + half)]
        return []

    def begin(self, q):
        for e in range(self.experts):
            self.across(q, 0, e, True).start()
        for k in range(self.experts):
            for s, e in self.pairs(k):
                self.direct(q, s, e).start()
        for e in range(self.experts):
            self.X[q, e, 0, : self.cap] = self.rows[q, e]

    def receive(self, q, *ks):
        for k in ks:
            for s, e in self.pairs(k):
                copy = self.onward(q, e) if s == 3 else self.direct(q, s, e)
                copy.wait_recv()
                self.across(q, s, e).start()
                if k < self.half:
                    self.onward(q, e).start()

    def matmuls(self, e, s, n):
        chunk, tall = self.chunk, n * 2 * self.cap
        inner = 0.0
        for q in range(2):
            block = self.X[q, e, s : s + n].reshape(tall, chunk)
            inner = inner + dot(block, self.W1[e, q * chunk : (q + 1) * chunk])
        hidden = jnp.maximum(inner, 0.0).astype(BF16)
        for q in range(2):
            sums = dot(hidden, self.W2[e, :, q * chunk : (q + 1) * chunk]).astype(BF16)
            self.PS[q, e, s : s + n] = sums.reshape(n, 2 * self.cap, chunk)

    def local(self):
        def one(e, carry):
            for copy in self.weights(e):
                copy.wait()
            for q in range(2):
                self.across(q, 0, e, True).wait_recv()
            self.matmuls(e, 0, 1)
            for q in range(2):
                self.part_across(q, 0, e).start()
            return carry

        lax.fori_loop(0, self.experts, one, 0)

    def compute(self, s, n, *es):
        for e in es:
            for i in range(n):
                for q in range(2):
                    self.across(q, s + i, e).wait_recv()
        first, gap = es[0], es[1] - es[0]

        def one(i, carry):
            self.matmuls(first + gap * i, s, n)
            return carry

        lax.fori_loop(0, 2, one, 0)
        for q in range(2):
            for e in es:
                for i in range(n):
                    self.part_across(q, s + i, e).start()

    def chip_sum(self, q, s, e):
        self.part_across(q, s, e).wait_recv()
        return self.PS[q, e, s, : self.cap].astype(F32) + self.R[q, e, s].astype(F32)

    def settle(self, s, n, *es):
        for q in range(2):
            self.settle_chunk(q, s, n, *es)

    def settle_chunk(self, q, s, n, *es):
        for e in es:
            for i in range(n):
                self.S[q, e, s + i] = self.chip_sum(q, s + i, e).astype(BF16)
                if s == 3:
                    self.transit(q, e).start()
                elif (s + i == 1) == (e < self.half):
                    self.final(q, s + i == 2, e).start()

    def pass_on(self, q):
        for k in range(self.half):
            for e, s in ((k, 2), (k + self.half, 1)):
                self.transit(q, e).wait_recv()
                self.S[q, e, s] = (self.S[q, e, s].astype(F32) + self.T[q, e].astype(F32)).astype(BF16)
                self.final(q, s == 2, e).start()

    def gates(self):
        chunk = self.chunk
        for e in range(self.experts):
            logits = 0.0
            for q in range(2):
                weight = self.router[e : e + 1, q * chunk : (q + 1) * chunk].astype(F32)
                logits = logits + jnp.sum(self.rows[q, e].astype(F32) * weight, axis=1, keepdims=True)
            self.GT[e] = jax.nn.sigmoid(logits)

    def finish(self, q, weighted):
        for e in range(self.experts):
            total = self.chip_sum(q, 0, e)
            for up in (True, False):
                self.final(q, up, e).wait_recv()
            total = total + self.F[q, 0, e].astype(F32) + self.F[q, 1, e].astype(F32)
            weighted[q, e] = (self.GT[e] * total).astype(BF16)

    def run(self):
        half = self.half
        early, late = range(0, self.experts, half), range(1, self.experts, half)
        self.local()
        self.receive(0, *range(2 * half, 3 * half))
        self.receive(1, *range(half + 1))
        self.compute(1, 2, *early)
        self.receive(1, half + 1)
        self.compute(1, 2, *late)
        self.settle(1, 2, *early)
        self.receive(1, *range(2 * half, 3 * half))
        self.compute(3, 1, *early)
        self.settle(1, 2, *late)
        self.compute(3, 1, *late)
        for q in range(2):
            self.settle_chunk(q, 3, 1, *early, *late)
        for q in range(2):
            self.pass_on(q)

    def drain(self):
        for q in range(2):
            for e in range(self.experts):
                self.direct(q, 1, e).wait_send()
                self.direct(q, 2, e).wait_send()
                self.onward(q, e).wait_send()
                self.final(q, True, e).wait_send()
                self.final(q, False, e).wait_send()
                self.transit(q, e).wait_send()
                for s in range(4):
                    self.across(q, s, e, s == 0).wait_send()
                    self.part_across(q, s, e).wait_send()

    @staticmethod
    def scratch(experts, cap, width, hidden):
        dma = pltpu.SemaphoreType.DMA
        chunk = width // 2
        return dict(
            X=pltpu.VMEM((2, experts, 4, 2 * cap, chunk), BF16),
            W1=pltpu.VMEM((experts, width, hidden), BF16),
            W2=pltpu.VMEM((experts, hidden, width), BF16),
            PS=pltpu.VMEM((2, experts, 4, 2 * cap, chunk), BF16),
            R=pltpu.VMEM((2, experts, 4, cap, chunk), BF16),
            S=pltpu.VMEM((2, experts, 4, cap, chunk), BF16),
            T=pltpu.VMEM((2, experts, cap, chunk), BF16),
            F=pltpu.VMEM((2, 2, experts, cap, chunk), BF16),
            GT=pltpu.VMEM((experts, cap, 1), F32),
            w_sem=dma((2, experts)),
            sendP=dma((2, 4, experts)),
            recvP=dma((2, 4, experts)),
            sendI=dma((2, 4, experts)),
            recvI=dma((2, 4, experts)),
            rsend=dma((2, 4, experts)),
            rrecv=dma((2, 4, experts)),
            fsend=dma((2, 2, experts)),
            frecv=dma((2, 2, experts)),
            tsend=dma((2, experts)),
            trecv=dma((2, experts)),
        )


class NoExperts:
    def __init__(self, rows):
        self.rows = rows

    def __getattr__(self, name):
        return lambda *_: []

    def finish(self, q, weighted):
        for e in range(self.rows.shape[1]):
            weighted[q, e] = self.rows[q, e]


def layer_kernel(
    names, with_experts, dat_count, tokens, gain, ids, picks, router, w1_hbm, w2_hbm, out, rows, weighted, *refs
):
    refs = dict(zip(names, refs))
    tok_rows, width = tokens.shape
    ex = Exchange({k: refs.pop(k) for k in Exchange.scratch(8, 8, 8)}, width)
    xp = Experts(refs, rows, router, w1_hbm, w2_hbm) if with_experts else NoExperts(rows)
    xp.load()
    barrier = pltpu.get_barrier_semaphore()
    others = ex.peers() + xp.peers()
    for other in others:
        pl.semaphore_signal(barrier, inc=1, device_id=other, device_id_type=MESH)
    ex.routes(ids, picks, tok_rows, picks.shape[0] * picks.shape[1], dat_count)
    ex.normalize(tokens, gain)
    pl.semaphore_wait(barrier, len(others))

    ex.open_codes()
    ex.open_ring(0, 1, 2)
    ex.select(0, 0)
    ex.code_hop(1)
    ex.hop(1, 0, 1)
    ex.open_ring(3)
    ex.select(0, 1, 7)
    ex.code_hop(2)
    ex.hop(2, 0, 1)
    ex.hop(1, 2)
    ex.relay(0, 0, 0)
    ex.select(0, 2, 6)
    ex.select(1, 0)
    ex.code_hop(3)
    ex.hop(3, 0, 1)
    ex.hop(1, 3)
    ex.relay(0, 0, 1, 7)
    ex.select(0, 3, 5)
    ex.select(1, 1, 7)
    ex.code_hop(4)
    ex.hop(4, 0, 1)
    ex.select(0, 4)
    ex.hop(2, 2, 3)
    ex.relay(0, 0, 2, 6)
    ex.relay(0, 0, 3, 5)
    ex.relay(0, 1, 0)
    ex.select(1, 2, 6)
    ex.relay(0, 1, 1, 7)
    ex.hop(3, 2, 3)
    ex.select(1, 3, 5)
    ex.compact(0, rows)
    xp.begin(0)
    ex.relay(0, 1, 2, 6)
    ex.hop(4, 2, 3)
    ex.select(1, 4)
    ex.relay(0, 1, 3, 5)
    xp.receive(0, 0, 1)
    ex.compact(1, rows)
    xp.begin(1)
    xp.receive(0, 2, 3)
    xp.gates()
    ex.expanders()
    xp.run()

    steps = [(s, q, js) for s, js in ((1, (5, 3)), (2, (6, 2)), (3, (7, 1)), (4, (0,))) for q in range(2)]

    def send_ahead(h):
        if h < len(steps):
            _, q, js = steps[h]
            ex.send_back(q, weighted, *js)

    xp.finish(0, weighted)
    ex.send_back(0, weighted, FAR)
    send_ahead(0)
    xp.finish(1, weighted)
    ex.send_back(1, weighted, FAR)
    send_ahead(1)
    ex.fold_far(0)
    ex.relay(1, 0, *steps[0][2])
    ex.fold_far(1)
    send_ahead(2)
    ex.drain(0)
    for h, (s, q, js) in enumerate(steps):
        if h + 1 < len(steps):
            ex.relay(1, steps[h + 1][1], *steps[h + 1][2])
        send_ahead(h + 3)
        if s < FAR:
            ex.fold_step(q, s)
        else:
            if q == 0:
                xp.drain()
            ex.fold_end(q, tokens, out)
    ex.drain(1)


def whole_layer(tokens, gain, ids, picks, router, inner_weight, outer_weight, dat_count, with_experts=True):
    tok_rows, width = tokens.shape
    experts, _, hidden = inner_weight.shape
    cap = picks.shape[1]
    vmem = pl.BlockSpec(memory_space=pltpu.VMEM)
    hbm = pl.BlockSpec(memory_space=pl.ANY)
    scratch = Exchange.scratch(tok_rows, width, experts * cap)
    if with_experts:
        scratch.update(Experts.scratch(experts, cap, width, hidden))
    slots = pltpu.VMEM((2, experts, cap, width // 2), BF16)
    return pl.pallas_call(
        functools.partial(layer_kernel, tuple(scratch), with_experts, dat_count),
        name="whole_layer",
        out_shape=jax.ShapeDtypeStruct((tok_rows, width), BF16),
        in_specs=[vmem] * 5 + [hbm] * 2,
        out_specs=vmem,
        scratch_shapes=[slots, slots] + list(scratch.values()),
        compiler_params=pltpu.CompilerParams(
            collective_id=0, has_side_effects=True, vmem_limit_bytes=60 * 1024 * 1024
        ),
    )(tokens, gain, ids, picks, router, inner_weight, outer_weight)


def body(tokens, norm_gain, router_weight, inner_weight, outer_weight, slot_tokens, slot_ids):
    return whole_layer(
        tokens, norm_gain[None, :], slot_ids.T, slot_tokens, router_weight.T, inner_weight, outer_weight,
        lax.axis_size("dat"),
    )


def solution(mesh):
    in_specs = (
        P(("exp", "dat"), None),
        P(),
        P(None, "exp"),
        P("exp", None, "dat"),
        P("exp", "dat", None),
        P("exp", "dat"),
        P(("exp", "dat"), None),
    )
    out_specs = P(("exp", "dat"), None)
    return jax.shard_map(body, mesh=mesh, in_specs=in_specs, out_specs=out_specs, check_vma=False)
```

time: 208 us -> 108 us (0.52)
  waiting for transfers between devices: 145 us -> 0 us
  Pallas kernels: 0 us -> 105 us
  starting transfers between devices: 21.2 us -> 0 us
  matrix products: 17.3 us -> 0 us
  between operations: 13.6 us -> 0.01 us
  other arithmetic: 4.93 us -> 0 us
  local copies, waits for them, and re-layouts: 4.75 us -> 1.67 us
    pallas_call x0 -> x1, Pallas kernels: none -> 105 us  [whole_layer(): pl.pallas_call(functools.partial(layer_kernel, tuple(scratch), with_exper...]
    all_to_all x2 -> x0, waiting for transfers between devices: 77.6 us -> none  [the longest x1 39.4 us: body(): lax.all_to_all(returning, 'exp', split_axis=0, concat_axis=0, tiled=True)]
    reduce_scatter x1 -> x0, waiting for transfers between devices: 36.9 us -> none  [body(): lax.psum_scatter(jnp.einsum('cef,efd->ced', hidden, outer_weight, preferr...]
    all_gather x1 -> x0, waiting for transfers between devices: 30.9 us -> none  [body(): lax.all_gather(gathered_rows, 'dat', axis=0, tiled=True)]
    all_to_all x2 -> x0, starting transfers between devices: 21.2 us -> none  [the longest x1 11.3 us: body(): lax.all_to_all(outgoing, 'exp', split_axis=0, concat_axis=0, tiled=True)]
    dot_general x5 -> x0, matrix products: 17.3 us -> none  [the longest x1 11.5 us: body(): jnp.einsum('cef,efd->ced', hidden, outer_weight, preferred_element_type=j...]
  transfers between devices with their start and end apart: 4 -> 0, of which waited for: 4 -> 0; matrix products, arithmetic and copies ran while one was open for 1% -> 0% of each run, Pallas kernels for 0% -> 0%
where the time goes in v3:
time: 108 us; the launch traced here: 107 us
  Pallas kernels  105 us (97%)
  local copies, waits for them, and re-layouts  1.67 us (2%)
    pallas_call x1, Pallas kernels, whole_layer(): pl.pallas_call(functools.partial(layer_kernel, tuple(scratch), with_exper...  105 us

profile of v3, /device:TPU:8, one launch (start us, length us, event | category | flops | bytes accessed | tf_op | source)
XLA Modules:
  0.0 106.6 jit_solution(641791653014386416)
XLA Ops:
  0.0 104.9 %whole_layer.1 = bf16[128,1024]{1,0:T(8,128)(2,1)} custom-call(bf16[128,1024]{1,0:T(8,128)(2,1)} %tokens.1, f32[1,1024]{1,0:T(1,128)} %bitcast.4, s32[2,128]{1,0:T(2,128)} %bitcast.5, s32[4,64]{1,0:T(4,128)} %picks.1, bf16[4,1024]{1,0:T(4,128)(2,1)} %bitcast.3, bf16[4,1024,512]{2,1,0:T(8,128)(2,1)} %w1_hbm.1, bf16[4,512,1024]{2,1,0:T(8,128)(2,1)} %w2_hbm.1), custom_call_target="tpu_custom_call" | custom-call | tf_op jit(solution)/shard_map/whole_layer/pallas_call | solution.py:647
  104.9 1.7 %copy.9 = bf16[128,1024]{1,0:T(8,128)(2,1)} copy(bf16[128,1024]{1,0:T(8,128)(2,1)} %whole_layer.1) | data formatting | bytes 524288

commit v4 on v3

--- a/solution.py
+++ b/solution.py
@@ -16,6 +16,7 @@
 NX, NZ, NY = 4, 8, 4
 BUCKET = 24
 FAR = NZ // 2
+NP = 8
 
 
 def dot(a, b):
@@ -39,6 +40,10 @@
     return pltpu.make_async_remote_copy(
         src_ref=src, dst_ref=dst, send_sem=send, recv_sem=recv, device_id=where, device_id_type=MESH
     )
+
+
+def pieces(q):
+    return list(range(q * NP // 2, (q + 1) * NP // 2))
 
 
 class Exchange:
@@ -46,7 +51,7 @@
         self.__dict__.update(refs)
         exp = lax.axis_index("exp")
         self.x, self.z = exp // NZ, exp % NZ
-        self.chunk, self.piece = width // 2, width // 4
+        self.chunk, self.piece = width // 2, width // NP
 
     def at(self, dx, dz):
         return {"exp": ((self.x + dx) % NX) * NZ + (self.z + dz) % NZ}
@@ -101,49 +106,27 @@
             if s < FAR - 1:
                 self.code(NZ - s - 1).start()
 
-    def bucket(self, ph, q, j, kind):
-        def place(i):
-            return self.A.at[q, i, j] if ph == 0 else self.B.at[q, j, i]
-
-        send, recv = self.xsend.at[ph, q, j, kind], self.xrecv.at[ph, q, j, kind]
-        up, down = self.at(1, 0), self.at(NX - 1, 0)
-        if kind == 0:
-            return remote(self.Q.at[ph, q, j, 0], place(3), send, recv, up)
-        if kind == 1:
-            return remote(self.Q.at[ph, q, j, 1], place(1), send, recv, down)
-        h = kind % 2
-        half = place(2).at[:, pl.ds(h * self.piece, self.piece)]
-        where = down if h else up
-        if kind >= 4:
-            return remote(self.TR.at[ph, q, j, h], half, send, recv, where)
-        if j == FAR:
-            return remote(self.QH.at[ph, q, j, h], half, send, recv, self.at(2, 0))
-        return remote(self.QH.at[ph, q, j, h], self.TR.at[ph, q, j, h], send, recv, where)
+    def bucket(self, ph, q, j, dx):
+        there = NX - dx
+        dst = self.A.at[q, there, j] if ph == 0 else self.B.at[q, j, there]
+        i = dx - 1
+        return remote(
+            self.Q.at[ph, q, j, i], dst, self.xsend.at[ph, q, j, i], self.xrecv.at[ph, q, j, i], self.at(dx, 0)
+        )
 
     def send_buckets(self, ph, q, j, rows):
         n = BUCKET
-        for h in range(2):
-            self.QH[ph, q, j, h] = rows[2 * n : 3 * n, h * self.piece : (h + 1) * self.piece]
-            self.bucket(ph, q, j, 2 + h).start()
-        self.Q[ph, q, j, 0] = rows[n : 2 * n]
-        self.bucket(ph, q, j, 0).start()
-        self.Q[ph, q, j, 1] = rows[3 * n :]
-        self.bucket(ph, q, j, 1).start()
+        for dx in (2, 1, 3):
+            self.Q[ph, q, j, dx - 1] = rows[dx * n : (dx + 1) * n]
+            self.bucket(ph, q, j, dx).start()
         if ph == 0:
             self.A[q, 0, j] = rows[:n]
         else:
             self.B[q, j, 0] = rows[:n]
 
-    def relay(self, ph, q, *js):
-        for j in js:
-            if j != FAR:
-                for h in range(2):
-                    self.bucket(ph, q, j, 2 + h).wait_recv()
-                    self.bucket(ph, q, j, 4 + h).start()
-
     def landed(self, ph, q, j):
-        for kind in (0, 1, 2, 3) if j == FAR else (0, 1, 4, 5):
-            self.bucket(ph, q, j, kind).wait_recv()
+        for dx in range(1, NX):
+            self.bucket(ph, q, j, dx).wait_recv()
 
     def row_codes(self, shape, dim):
         line = lax.broadcasted_iota(I32, shape, dim)
@@ -155,14 +138,14 @@
         for j in js:
             rows = self.row_codes((NX * BUCKET, self.C.shape[2]), 0)
             hit = onehot((rows == self.C[j, 0:1]) | (rows == self.C[j, 1:2]))
-            parts = [dot(hit, self.G[j, 2 * q + h]) for h in range(2)]
+            parts = [dot(hit, self.G[j, p]) for p in pieces(q)]
             self.send_buckets(0, q, j, jnp.concatenate(parts, axis=1).astype(BF16))
 
     def normalize(self, tokens, gain):
         values = tokens[...].astype(F32)
         scale = lax.rsqrt(jnp.mean(values * values, axis=-1, keepdims=True) + EPSILON)
         normed = (values * scale * gain[...]).astype(BF16)
-        for p in range(4):
+        for p in range(NP):
             self.G[0, p] = normed[:, p * self.piece : (p + 1) * self.piece]
 
     def open_ring(self, *ps):
@@ -215,7 +198,7 @@
             self.send_buckets(1, q, j, out.astype(BF16))
 
     def part(self, j, p):
-        q, h = p // 2, p % 2
+        q, h = p // (NP // 2), p % (NP // 2)
         n = NX * BUCKET
         rows = self.B[q, j, :, :, h * self.piece : (h + 1) * self.piece].reshape(n, self.piece)
         return dot(self.OT[j][:, :n], rows)
@@ -240,22 +223,21 @@
 
     def fold_far(self, q):
         self.landed(1, q, FAR)
-        self.emit(FAR, 2 * q, True, False)
-        self.emit(FAR, 2 * q + 1, False, False)
+        for p in pieces(q):
+            self.emit(FAR, p, p % 2 == 0, False)
 
     def fold_step(self, q, s):
         up, down = FAR + s, FAR - s
-        even, odd = 2 * q, 2 * q + 1
         for j in (up, down):
             self.landed(1, q, j)
-        self.emit(up, odd, True, s > 1)
-        self.emit(down, even, False, s > 1)
-        self.emit(up, even, True, True)
-        self.emit(down, odd, False, True)
+        for first in (True, False):
+            for p in pieces(q):
+                rising = (p % 2 == 1) == first
+                self.emit(up if rising else down, p, rising, s > 1 or not first)
 
     def fold_end(self, q, tokens, out):
         self.landed(1, q, 0)
-        for p in (2 * q, 2 * q + 1):
+        for p in pieces(q):
             cut = slice(p * self.piece, (p + 1) * self.piece)
             total = tokens[:, cut].astype(F32) + self.part(0, p)
             total = total + self.carried(0, p, True) + self.carried(0, p, False)
@@ -264,12 +246,12 @@
     def drain(self, ph):
         for q in range(2):
             for j in range(NZ):
-                for kind in range(4 if j == FAR else 6):
-                    self.bucket(ph, q, j, kind).wait_send()
+                for dx in range(1, NX):
+                    self.bucket(ph, q, j, dx).wait_send()
         for j in range(1, NZ):
             if ph == 0:
                 self.code(j).wait_send()
-            for p in range(4):
+            for p in range(NP):
                 far_up = j == FAR and p % 2 == 0
                 if ph == 0:
                     self.spread(j, p, j < FAR or far_up).wait_send()
@@ -279,27 +261,25 @@
     @staticmethod
     def scratch(tok_rows, width, slots):
         dma = pltpu.SemaphoreType.DMA
-        chunk, piece = width // 2, width // 4
+        chunk, piece = width // 2, width // NP
         return dict(
-            G=pltpu.VMEM((NZ, 4, tok_rows, piece), BF16),
+            G=pltpu.VMEM((NZ, NP, tok_rows, piece), BF16),
             C=pltpu.VMEM((NZ, 2, tok_rows), I32),
             PO=pltpu.VMEM((2, slots // 2), I32),
-            Q=pltpu.VMEM((2, 2, NZ, 2, BUCKET, chunk), BF16),
-            QH=pltpu.VMEM((2, 2, NZ, 2, BUCKET, piece), BF16),
-            TR=pltpu.VMEM((2, 2, NZ, 2, BUCKET, piece), BF16),
+            Q=pltpu.VMEM((2, 2, NZ, NX - 1, BUCKET, chunk), BF16),
             A=pltpu.VMEM((2, NX, NZ, BUCKET, chunk), BF16),
             B=pltpu.VMEM((2, NZ, NX, BUCKET, chunk), BF16),
             OT=pltpu.VMEM((NZ, tok_rows, 128), BF16),
-            V=pltpu.VMEM((NZ, 4, tok_rows, piece), BF16),
-            RP=pltpu.VMEM((2, NZ, 4, tok_rows, piece), BF16),
-            gsend=dma((NZ, 4)),
-            grecv=dma((NZ, 4)),
+            V=pltpu.VMEM((NZ, NP, tok_rows, piece), BF16),
+            RP=pltpu.VMEM((2, NZ, NP, tok_rows, piece), BF16),
+            gsend=dma((NZ, NP)),
+            grecv=dma((NZ, NP)),
             csend=dma((NZ,)),
             crecv=dma((NZ,)),
-            xsend=dma((2, 2, NZ, 6)),
-            xrecv=dma((2, 2, NZ, 6)),
-            vsend=dma((NZ, 4)),
-            vrecv=dma((2, NZ, 4)),
+            xsend=dma((2, 2, NZ, NX - 1)),
+            xrecv=dma((2, 2, NZ, NX - 1)),
+            vsend=dma((NZ, NP)),
+            vrecv=dma((2, NZ, NP)),
         )
 
 
@@ -434,11 +414,7 @@
         self.part_across(q, s, e).wait_recv()
         return self.PS[q, e, s, : self.cap].astype(F32) + self.R[q, e, s].astype(F32)
 
-    def settle(self, s, n, *es):
-        for q in range(2):
-            self.settle_chunk(q, s, n, *es)
-
-    def settle_chunk(self, q, s, n, *es):
+    def settle(self, q, s, n, *es):
         for e in es:
             for i in range(n):
                 self.S[q, e, s + i] = self.chip_sum(q, s + i, e).astype(BF16)
@@ -476,19 +452,21 @@
         early, late = range(0, self.experts, half), range(1, self.experts, half)
         self.local()
         self.receive(0, *range(2 * half, 3 * half))
-        self.receive(1, *range(half + 1))
+        self.receive(1, *range(2 * half))
         self.compute(1, 2, *early)
-        self.receive(1, half + 1)
         self.compute(1, 2, *late)
-        self.settle(1, 2, *early)
+        self.settle(0, 1, 2, *early)
         self.receive(1, *range(2 * half, 3 * half))
+        self.settle(0, 1, 2, *late)
         self.compute(3, 1, *early)
-        self.settle(1, 2, *late)
+        self.settle(1, 1, 2, *early)
         self.compute(3, 1, *late)
-        for q in range(2):
-            self.settle_chunk(q, 3, 1, *early, *late)
-        for q in range(2):
-            self.pass_on(q)
+        self.settle(0, 3, 1, *early)
+        self.settle(0, 3, 1, *late)
+        self.settle(1, 1, 2, *late)
+        self.pass_on(0)
+        self.settle(1, 3, 1, *early)
+        self.settle(1, 3, 1, *late)
 
     def drain(self):
         for q in range(2):
@@ -559,42 +537,35 @@
     ex.normalize(tokens, gain)
     pl.semaphore_wait(barrier, len(others))
 
+    near, rest = pieces(0), pieces(1)
     ex.open_codes()
-    ex.open_ring(0, 1, 2)
+    ex.open_ring(*near, *rest[:2])
     ex.select(0, 0)
     ex.code_hop(1)
-    ex.hop(1, 0, 1)
-    ex.open_ring(3)
+    ex.hop(1, *near)
+    ex.open_ring(*rest[2:])
     ex.select(0, 1, 7)
     ex.code_hop(2)
-    ex.hop(2, 0, 1)
-    ex.hop(1, 2)
-    ex.relay(0, 0, 0)
+    ex.hop(2, *near)
+    ex.hop(1, *rest[:2])
     ex.select(0, 2, 6)
     ex.select(1, 0)
     ex.code_hop(3)
-    ex.hop(3, 0, 1)
-    ex.hop(1, 3)
-    ex.relay(0, 0, 1, 7)
+    ex.hop(3, *near)
+    ex.hop(1, *rest[2:])
     ex.select(0, 3, 5)
     ex.select(1, 1, 7)
     ex.code_hop(4)
-    ex.hop(4, 0, 1)
+    ex.hop(4, *near)
     ex.select(0, 4)
-    ex.hop(2, 2, 3)
-    ex.relay(0, 0, 2, 6)
-    ex.relay(0, 0, 3, 5)
-    ex.relay(0, 1, 0)
+    ex.hop(2, *rest)
     ex.select(1, 2, 6)
-    ex.relay(0, 1, 1, 7)
-    ex.hop(3, 2, 3)
+    ex.hop(3, *rest)
     ex.select(1, 3, 5)
     ex.compact(0, rows)
     xp.begin(0)
-    ex.relay(0, 1, 2, 6)
-    ex.hop(4, 2, 3)
+    ex.hop(4, *rest)
     ex.select(1, 4)
-    ex.relay(0, 1, 3, 5)
     xp.receive(0, 0, 1)
     ex.compact(1, rows)
     xp.begin(1)
@@ -603,34 +574,29 @@
     ex.expanders()
     xp.run()
 
-    steps = [(s, q, js) for s, js in ((1, (5, 3)), (2, (6, 2)), (3, (7, 1)), (4, (0,))) for q in range(2)]
-
-    def send_ahead(h):
-        if h < len(steps):
-            _, q, js = steps[h]
-            ex.send_back(q, weighted, *js)
-
     xp.finish(0, weighted)
-    ex.send_back(0, weighted, FAR)
-    send_ahead(0)
+    ex.send_back(0, weighted, FAR, 5, 3)
+    xp.pass_on(1)
+    ex.fold_far(0)
+    ex.send_back(0, weighted, 6, 2)
     xp.finish(1, weighted)
-    ex.send_back(1, weighted, FAR)
-    send_ahead(1)
-    ex.fold_far(0)
-    ex.relay(1, 0, *steps[0][2])
+    ex.send_back(1, weighted, FAR, 5, 3)
+    ex.fold_step(0, 1)
     ex.fold_far(1)
-    send_ahead(2)
+    ex.send_back(0, weighted, 7, 1)
+    ex.fold_step(0, 2)
+    ex.send_back(1, weighted, 6, 2)
+    ex.fold_step(1, 1)
+    ex.send_back(0, weighted, 0)
+    ex.fold_step(0, 3)
+    ex.send_back(1, weighted, 7, 1)
     ex.drain(0)
-    for h, (s, q, js) in enumerate(steps):
-        if h + 1 < len(steps):
-            ex.relay(1, steps[h + 1][1], *steps[h + 1][2])
-        send_ahead(h + 3)
-        if s < FAR:
-            ex.fold_step(q, s)
-        else:
-            if q == 0:
-                xp.drain()
-            ex.fold_end(q, tokens, out)
+    ex.fold_step(1, 2)
+    ex.send_back(1, weighted, 0)
+    xp.drain()
+    ex.fold_end(0, tokens, out)
+    ex.fold_step(1, 3)
+    ex.fold_end(1, tokens, out)
     ex.drain(1)
 
 

time: 108 us -> 105 us (0.972)
  Pallas kernels: 105 us -> 103 us
    pallas_call x1, Pallas kernels: 105 us -> 103 us  [whole_layer(): pl.pallas_call(functools.partial(layer_kernel, tuple(scratch), with_exper...]
where the time goes in v4:
time: 105 us
  Pallas kernels  103 us (98%)
  local copies, waits for them, and re-layouts  1.67 us (2%)
    pallas_call x1, Pallas kernels, whole_layer(): pl.pallas_call(functools.partial(layer_kernel, tuple(scratch), with_exper...  103 us

profile of v4, /device:TPU:8, one launch (start us, length us, event | category | flops | bytes accessed | tf_op | source)
XLA Modules:
  0.0 104.6 jit_solution(11647638580725708184)
XLA Ops:
  0.0 102.9 %whole_layer.1 = bf16[128,1024]{1,0:T(8,128)(2,1)} custom-call(bf16[128,1024]{1,0:T(8,128)(2,1)} %tokens.1, f32[1,1024]{1,0:T(1,128)} %bitcast.4, s32[2,128]{1,0:T(2,128)} %bitcast.5, s32[4,64]{1,0:T(4,128)} %picks.1, bf16[4,1024]{1,0:T(4,128)(2,1)} %bitcast.3, bf16[4,1024,512]{2,1,0:T(8,128)(2,1)} %w1_hbm.1, bf16[4,512,1024]{2,1,0:T(8,128)(2,1)} %w2_hbm.1), custom_call_target="tpu_custom_call" | custom-call | tf_op jit(solution)/shard_map/whole_layer/pallas_call | solution.py:613
  102.9 1.7 %copy.9 = bf16[128,1024]{1,0:T(8,128)(2,1)} copy(bf16[128,1024]{1,0:T(8,128)(2,1)} %whole_layer.1) | data formatting | bytes 524288

commit v5 on v4

--- a/solution.py
+++ b/solution.py
@@ -460,8 +460,8 @@
         self.settle(0, 1, 2, *late)
         self.compute(3, 1, *early)
         self.settle(1, 1, 2, *early)
+        self.settle(0, 3, 1, *early)
         self.compute(3, 1, *late)
-        self.settle(0, 3, 1, *early)
         self.settle(0, 3, 1, *late)
         self.settle(1, 1, 2, *late)
         self.pass_on(0)
@@ -564,6 +564,7 @@
     ex.select(1, 3, 5)
     ex.compact(0, rows)
     xp.begin(0)
+    ex.expanders()
     ex.hop(4, *rest)
     ex.select(1, 4)
     xp.receive(0, 0, 1)
@@ -571,7 +572,6 @@
     xp.begin(1)
     xp.receive(0, 2, 3)
     xp.gates()
-    ex.expanders()
     xp.run()
 
     xp.finish(0, weighted)
@@ -582,22 +582,22 @@
     xp.finish(1, weighted)
     ex.send_back(1, weighted, FAR, 5, 3)
     ex.fold_step(0, 1)
+    ex.send_back(0, weighted, 7, 1)
     ex.fold_far(1)
-    ex.send_back(0, weighted, 7, 1)
+    ex.send_back(1, weighted, 6, 2)
     ex.fold_step(0, 2)
-    ex.send_back(1, weighted, 6, 2)
+    ex.send_back(0, weighted, 0)
     ex.fold_step(1, 1)
-    ex.send_back(0, weighted, 0)
+    ex.send_back(1, weighted, 7, 1)
     ex.fold_step(0, 3)
-    ex.send_back(1, weighted, 7, 1)
+    ex.send_back(1, weighted, 0)
     ex.drain(0)
     ex.fold_step(1, 2)
-    ex.send_back(1, weighted, 0)
     xp.drain()
     ex.fold_end(0, tokens, out)
     ex.fold_step(1, 3)
+    ex.drain(1)
     ex.fold_end(1, tokens, out)
-    ex.drain(1)
 
 
 def whole_layer(tokens, gain, ids, picks, router, inner_weight, outer_weight, dat_count, with_experts=True):

time: 105 us -> 105 us (level)
  no operation moved by 1% of the time
where the time goes in v5:
time: 105 us
  Pallas kernels  103 us (98%)
  local copies, waits for them, and re-layouts  1.67 us (2%)
    pallas_call x1, Pallas kernels, whole_layer(): pl.pallas_call(functools.partial(layer_kernel, tuple(scratch), with_exper...  103 us

profile of v5, /device:TPU:8, one launch (start us, length us, event | category | flops | bytes accessed | tf_op | source)
XLA Modules:
  0.0 104.5 jit_solution(14105775996956941833)
XLA Ops:
  0.0 102.8 %whole_layer.1 = bf16[128,1024]{1,0:T(8,128)(2,1)} custom-call(bf16[128,1024]{1,0:T(8,128)(2,1)} %tokens.1, f32[1,1024]{1,0:T(1,128)} %bitcast.4, s32[2,128]{1,0:T(2,128)} %bitcast.5, s32[4,64]{1,0:T(4,128)} %picks.1, bf16[4,1024]{1,0:T(4,128)(2,1)} %bitcast.3, bf16[4,1024,512]{2,1,0:T(8,128)(2,1)} %w1_hbm.1, bf16[4,512,1024]{2,1,0:T(8,128)(2,1)} %w2_hbm.1), custom_call_target="tpu_custom_call" | custom-call | tf_op jit(solution)/shard_map/whole_layer/pallas_call | solution.py:613
  102.9 1.7 %copy.9 = bf16[128,1024]{1,0:T(8,128)(2,1)} copy(bf16[128,1024]{1,0:T(8,128)(2,1)} %whole_layer.1) | data formatting | bytes 524288
